TPU v7x, 32 devices: a whole 2x2x4 slice. The times are simulated.
32 devices in a mesh: vp: 32 (over z, y, x, core).
Axes of the slice: x: 2, y: 2, z: 4, core: 2. Of those that a mesh axis runs over, the one named last changes fastest.
Arguments:
- table_in: float32 [49152, 576], P('vp')
- table_out: float32 [49152, 576], P('vp')
- center_ids: int32 [131072], P('vp')
- context_ids: int32 [131072], P('vp')
- negative_ids: int32 [65536], P('vp')
Outputs:
- output 1: float32 [49152, 576], P('vp')
- output 2: float32 [49152, 576], P('vp')
All inputs are finite; a program needn't handle non-finite values.
Results may differ from a plain program's by a relative error of at most 0.001.
Values sent between devices are 32-bit elements.
A program may use at most 1 GiB of HBM per device.

v0:
```python
import jax
import jax.numpy as jnp
from jax import lax
from jax.sharding import PartitionSpec as P

LEARN_RATE = 1.0
NEG_WEIGHT = 5.0
AXIS_NAME = 'vp'


def list_capacity(num_ids, shards):
    common_slots = 3 * num_ids // shards
    return common_slots + (num_ids - common_slots + shards - 1) // shards


def send_layout(id_list, shard_rows, shards, capacity):
    num_ids = id_list.shape[0]
    owner_idx = id_list // shard_rows
    sort_order = jnp.argsort(owner_idx, stable=True).astype(jnp.int32)
    owner_sorted = owner_idx[sort_order]
    per_owner = jax.ops.segment_sum(jnp.ones_like(owner_idx), owner_idx, num_segments=shards)
    owner_start = jnp.cumsum(per_owner) - per_owner
    cell_sorted = owner_sorted * capacity + jnp.arange(num_ids, dtype=jnp.int32) - owner_start[owner_sorted]
    cell_of_id = jnp.zeros_like(id_list).at[sort_order].set(cell_sorted)
    slot_of_cell = jnp.full((shards * capacity,), num_ids, jnp.int32).at[cell_sorted].set(sort_order)
    filler = (jnp.arange(shards * capacity, dtype=jnp.int32) // capacity) * shard_rows
    id_of_cell = jnp.take(id_list, slot_of_cell, axis=0, mode='fill', fill_value=-1)
    id_of_cell = jnp.where(slot_of_cell < num_ids, id_of_cell, filler)
    return cell_of_id, slot_of_cell, id_of_cell


def fetch_rows(table_shard, id_of_cell, shards, capacity):
    ids_asked = lax.all_to_all(id_of_cell.reshape(shards, capacity), AXIS_NAME, 0, 0)
    local_rows = ids_asked - lax.axis_index(AXIS_NAME) * table_shard.shape[0]
    rows_found = jnp.take(table_shard, local_rows, axis=0)
    returned = lax.all_to_all(rows_found, AXIS_NAME, 0, 0)
    return local_rows.reshape(-1), returned.reshape(shards * capacity, table_shard.shape[1])


def send_grads(grad_cells, local_rows, shards, capacity, shard_rows):
    arrived = lax.all_to_all(grad_cells.reshape(shards, capacity, -1), AXIS_NAME, 0, 0)
    return jax.ops.segment_sum(arrived.reshape(shards * capacity, -1), local_rows, num_segments=shard_rows)


def pair_grads(center_vec, context_vec, negative_vec):
    neg_scale = NEG_WEIGHT / negative_vec.shape[0]
    pos_score = jnp.sum(center_vec * context_vec, axis=1)
    center_half = center_vec.astype(jnp.bfloat16)
    negative_half = negative_vec.astype(jnp.bfloat16)
    neg_score = lax.dot_general(center_half, negative_half, (((1,), (1,)), ((), ())), preferred_element_type=jnp.float32)
    pos_grad = (jax.nn.sigmoid(pos_score) - 1.0)[:, None]
    neg_grad = (neg_scale * jax.nn.sigmoid(neg_score)).astype(jnp.bfloat16)
    d_center = pos_grad * context_vec + jnp.dot(neg_grad, negative_half, preferred_element_type=jnp.float32)
    d_context = pos_grad * center_vec
    d_negative = lax.dot_general(neg_grad, center_half, (((0,), (0,)), ((), ())), preferred_element_type=jnp.float32)
    return d_center, d_context, d_negative


def solution(mesh):
    shards = mesh.shape[AXIS_NAME]

    def device_step(in_shard, out_shard, center_ids, context_ids, negative_ids):
        shard_rows = in_shard.shape[0]
        pairs_dev = center_ids.shape[0]
        cap_pairs = list_capacity(pairs_dev, shards)
        cap_out = cap_pairs + list_capacity(negative_ids.shape[0], shards)
        out_ids = jnp.concatenate([context_ids, negative_ids])
        in_cell, in_slot, in_asks = send_layout(center_ids, shard_rows, shards, cap_pairs)
        out_cell, out_slot, out_asks = send_layout(out_ids, shard_rows, shards, cap_out)
        in_local, in_rows = fetch_rows(in_shard, in_asks, shards, cap_pairs)
        out_local, out_rows = fetch_rows(out_shard, out_asks, shards, cap_out)
        center_vec = jnp.take(in_rows, in_cell, axis=0)
        looked_up = jnp.take(out_rows, out_cell, axis=0)
        d_center, d_context, d_negative = pair_grads(center_vec, looked_up[:pairs_dev], looked_up[pairs_dev:])
        in_cells = jnp.take(d_center, in_slot, axis=0, mode='fill', fill_value=0.0)
        out_cells = jnp.take(jnp.concatenate([d_context, d_negative]), out_slot, axis=0, mode='fill', fill_value=0.0)
        in_sum = send_grads(in_cells, in_local, shards, cap_pairs, shard_rows)
        out_sum = send_grads(out_cells, out_local, shards, cap_out, shard_rows)
        return in_shard - LEARN_RATE * in_sum, out_shard - LEARN_RATE * out_sum

    return jax.shard_map(device_step, mesh=mesh, in_specs=(P(AXIS_NAME, None), P(AXIS_NAME, None), P(AXIS_NAME), P(AXIS_NAME), P(AXIS_NAME)), out_specs=(P(AXIS_NAME, None), P(AXIS_NAME, None)), check_vma=False)
```

profile of v0, /device:TPU:24, one launch (start us, length us, event | category | flops | bytes accessed | tf_op | source)
XLA Modules:
  0.0 5529.4 jit_solution(16360506758016585721)
XLA Ops:
  99.1 82.3 %gather_fusion.1 = s32[16000]{0:T(1024)S(1)} fusion(s32[4096]{0:T(1024)S(1)} %copy-done, s32[16384]{0:T(1024)S(1)} %pad_clamp_fusion.3), kind=kCustom, calls=%fused_computation.1 | custom fusion | bytes 192000 | tf_op jit(solution)/shard_map/jit(_take)/gather | solution.py:27
  188.3 43.3 scatter_custom_fusion.3
  320.5 123.2 %gather_fusion.5 = s32[24000]{0:T(1024)S(1)} fusion(s32[6144]{0:T(1024)S(1)} %constant_dynamic-update-slice_fusion, s32[24576]{0:T(1024)S(1)} %pad_clamp_fusion.1), kind=kCustom, calls=%fused_computation.5 | custom fusion | bytes 288000 | tf_op jit(solution)/shard_map/jit(_take)/gather | solution.py:27
  456.5 54.0 gather_fusion.2
  637.3 78.9 %gather_fusion.6 = f32[24000,576]{1,0:T(8,128)} fusion(f32[1536,576]{1,0:T(8,128)} %copy.69, s32[24576]{0:T(1024)S(1)} %pad_clamp_fusion), kind=kCustom, calls=%fused_computation.6 | custom fusion | bytes 110688000 | tf_op jit(solution)/shard_map/jit(_take)/gather | solution.py:35
  716.2 57.0 %reshape.782 = f32[32,750,576]{2,1,0:T(8,128)} reshape(f32[24000,576]{1,0:T(8,128)} %gather_fusion.6) | data formatting | bytes 110592000 | tf_op jit(solution)/shard_map/jit(_take)/gather | solution.py:35
  773.2 60.8 %copy.91 = f32[32,750,576]{1,0,2:T(8,128)} copy(f32[32,750,576]{2,1,0:T(8,128)} %reshape.782) | data formatting | bytes 110592000 | tf_op jit(solution)/shard_map/jit(_take)/gather | solution.py:35
  911.6 531.2 %all-to-all-done.1 = f32[32,500,576]{1,2,0:T(8,128)} async-done(((f32[32,500,576]{1,2,0:T(8,128)}), f32[32,500,576]{1,2,0:T(8,128)}, u32[]{:S(2)}, u32[]{:S(2)}) %all-to-all-start.1) | async-done | bytes 36864032 | tf_op jit(solution)/shard_map/all_to_all | solution.py:36
  1633.7 1065.0 %all-to-all-done.3 = f32[32,750,576]{1,2,0:T(8,128)} async-done(((f32[32,750,576]{1,2,0:T(8,128)}), f32[32,750,576]{1,2,0:T(8,128)}, u32[]{:S(2)}, u32[]{:S(2)}) %all-to-all-start.3) | async-done | bytes 55296032 | tf_op jit(solution)/shard_map/all_to_all | solution.py:36
  2698.7 54.3 copy.92
  2753.0 56.9 %reshape.783 = f32[24000,576]{1,0:T(8,128)} reshape(f32[32,750,576]{2,1,0:T(8,128)} %copy.92) | data formatting | bytes 110592000 | tf_op jit(solution)/shard_map/reshape | solution.py:37
  2810.0 46.5 gather_fusion.7
  2949.1 55.8 %gather_fusion.8 = f32[16000,576]{1,0:T(8,128)} fusion(f32[4096,576]{1,0:T(8,128)} %copy.75, s32[16384]{0:T(1024)S(1)} %copy-done.12), kind=kCustom, calls=%fused_computation.8 | custom fusion | bytes 73792000 | tf_op jit(solution)/shard_map/jit(_take)/gather | solution.py:75
  3036.8 42.0 copy.93
  3117.6 52.9 all-to-all-start.4
  3217.6 82.2 %gather_fusion.9 = f32[24000,576]{1,0:T(8,128)} fusion(f32[6144,576]{1,0:T(8,128)} %copy.81, s32[24576]{0:T(1024)S(1)} %copy-done.8), kind=kCustom, calls=%fused_computation.9 | custom fusion | bytes 110688000 | tf_op jit(solution)/shard_map/jit(_take)/gather | solution.py:76
  3299.9 57.0 %reshape.786 = f32[32,750,576]{2,1,0:T(8,128)} reshape(f32[24000,576]{1,0:T(8,128)} %gather_fusion.9) | data formatting | bytes 110592000 | tf_op jit(solution)/shard_map/jit(_take)/gather | solution.py:76
  3356.8 60.8 %copy.95 = f32[32,750,576]{1,0,2:T(8,128)} copy(f32[32,750,576]{2,1,0:T(8,128)} %reshape.786) | data formatting | bytes 110592000 | tf_op jit(solution)/shard_map/jit(_take)/gather | solution.py:76
  3495.2 488.6 %all-to-all-done.4 = f32[32,500,576]{1,2,0:T(8,128)} async-done(((f32[32,500,576]{1,2,0:T(8,128)}), f32[32,500,576]{1,2,0:T(8,128)}, u32[]{:S(2)}, u32[]{:S(2)}) %all-to-all-start.4) | async-done | bytes 36864032 | tf_op jit(solution)/shard_map/all_to_all | solution.py:41
  4092.3 114.5 %scatter_custom_fusion.6 = f32[1536,576]{1,0:T(8,128)} fusion(s32[16000]{0:T(1024)S(1)} %reshape.597, f32[16000,576]{1,0:T(8,128)} %reshape.785, f32[]{:T(128)} %constant.107.clone.1), kind=kCustom, calls=%fused_computation.32 | custom fusion | flops 9216000 | bytes 3539456 | tf_op jit(solution)/shard_map/scatter-add | solution.py:42
  4217.6 1022.4 %all-to-all-done.5 = f32[32,750,576]{1,2,0:T(8,128)} async-done(((f32[32,750,576]{1,2,0:T(8,128)}), f32[32,750,576]{1,2,0:T(8,128)}, u32[]{:S(2)}, u32[]{:S(2)}) %all-to-all-start.5) | async-done | bytes 55296032 | tf_op jit(solution)/shard_map/all_to_all | solution.py:41
  5240.0 54.3 copy.96
  5294.3 56.9 %reshape.787 = f32[24000,576]{1,0:T(8,128)} reshape(f32[32,750,576]{2,1,0:T(8,128)} %copy.96) | data formatting | bytes 110592000 | tf_op jit(solution)/shard_map/reshape | solution.py:42
  5351.2 166.8 %scatter_custom_fusion.7 = f32[1536,576]{1,0:T(8,128)} fusion(s32[24000]{0:T(1024)S(1)} %reshape.605, f32[24000,576]{1,0:T(8,128)} %reshape.787, f32[]{:T(128)} %constant.107.clone.1), kind=kCustom, calls=%fused_computation.30 | custom fusion | flops 13824000 | bytes 3539456 | tf_op jit(solution)/shard_map/scatter-add | solution.py:42
  (162 shorter events, 1020.0 us)
Async XLA Ops:
  0.6 98.4 %copy-start = (s32[4096]{0:T(1024)S(1)}, s32[4096]{0:T(1024)}, u32[]{:S(2)}) copy-start(s32[4096]{0:T(1024)} %param.7) | copy-start | bytes 49156
  99.0 82.4 %copy-start.3 = (s32[16000]{0:T(1024)}, s32[16000]{0:T(1024)S(1)}, u32[]{:S(2)}) copy-start(s32[16000]{0:T(1024)S(1)} %scatter_custom_fusion.1) | copy-start | bytes 192004
  99.0 82.4 %copy-start.11 = (s32[16384]{0:T(1024)}, s32[16384]{0:T(1024)S(1)}, u32[]{:S(2)}) copy-start(s32[16384]{0:T(1024)S(1)} %pad_clamp_fusion.3) | copy-start | bytes 196612
  99.0 89.1 %copy-start.16 = (s32[4096]{0:T(1024)S(1)}, s32[4096]{0:T(1024)}, u32[]{:S(2)}) copy-start(s32[4096]{0:T(1024)} %param.8) | copy-start | bytes 49156
  99.1 89.1 %copy-start.21 = (s32[2048]{0:T(1024)S(1)}, s32[2048]{0:T(1024)}, u32[]{:S(2)}) copy-start(s32[2048]{0:T(1024)} %param.9) | copy-start | bytes 24580
  182.3 267.6 %all-to-all-start = ((s32[32,1,500]{2,1,0:T(1,128)}), s32[32,1,500]{2,1,0:T(1,128)S(1)}, u32[]{:S(2)}, u32[]{:S(2)}) async-start(s32[32,1,500]{2,1,0:T(1,128)} %all_to_all.24), calls=%async_computation | async-start | bytes 131072 | tf_op jit(solution)/shard_map/all_to_all | solution.py:33
  320.5 123.3 %copy-start.1 = (s32[24000]{0:T(1024)}, s32[24000]{0:T(1024)S(1)}, u32[]{:S(2)}) copy-start(s32[24000]{0:T(1024)S(1)} %scatter_custom_fusion.5) | copy-start | bytes 288004
  320.5 123.2 %copy-start.7 = (s32[24576]{0:T(1024)}, s32[24576]{0:T(1024)S(1)}, u32[]{:S(2)}) copy-start(s32[24576]{0:T(1024)S(1)} %pad_clamp_fusion.1) | copy-start | bytes 294916
  449.9 173.3 %all-to-all-start.2 = ((s32[32,1,750]{2,1,0:T(1,128)}), s32[32,1,750]{2,1,0:T(1,128)}, u32[]{:S(2)}, u32[]{:S(2)}) async-start(s32[32,1,750]{2,1,0:T(1,128)} %all_to_all.27), calls=%async_computation.2 | async-start | bytes 196608 | tf_op jit(solution)/shard_map/all_to_all | solution.py:33
  456.4 128.0 %copy-start.9 = (s32[32,1,500]{2,1,0:T(1,128)}, s32[32,1,500]{2,1,0:T(1,128)S(1)}, u32[]{:S(2)}) copy-start(s32[32,1,500]{2,1,0:T(1,128)S(1)} %get-tuple-element.67) | copy-start | bytes 192004
  623.2 819.6 %all-to-all-start.1 = ((f32[32,500,576]{1,2,0:T(8,128)}), f32[32,500,576]{1,2,0:T(8,128)}, u32[]{:S(2)}, u32[]{:S(2)}) async-start(f32[32,500,576]{1,2,0:T(8,128)} %copy.64), calls=%async_computation.1 | async-start | bytes 75497472 | tf_op jit(solution)/shard_map/all_to_all | solution.py:36
  773.2 60.8 %copy-start.6 = (s32[32,1,750]{2,1,0:T(1,128)S(1)}, s32[32,1,750]{2,1,0:T(1,128)}, u32[]{:S(2)}) copy-start(s32[32,1,750]{2,1,0:T(1,128)} %copy-done.5) | copy-start | bytes 288004
  911.6 566.3 %copy-start.4 = (s32[16000]{0:T(1024)S(1)}, s32[16000]{0:T(1024)}, u32[]{:S(2)}) copy-start(s32[16000]{0:T(1024)} %copy-done.3) | copy-start | bytes 192004
  1442.8 1255.9 %all-to-all-start.3 = ((f32[32,750,576]{1,2,0:T(8,128)}), f32[32,750,576]{1,2,0:T(8,128)}, u32[]{:S(2)}, u32[]{:S(2)}) async-start(f32[32,750,576]{1,2,0:T(8,128)} %copy.71), calls=%async_computation.3 | async-start | bytes 113246208 | tf_op jit(solution)/shard_map/all_to_all | solution.py:36
  2918.1 20.3 copy-start.17
  3036.8 42.0 copy-start.15
  3117.6 52.9 copy-start.2
  3117.6 53.8 copy-start.18
  3117.6 53.8 copy-start.20
  3117.6 866.2 %all-to-all-start.4 = ((f32[32,500,576]{1,2,0:T(8,128)}), f32[32,500,576]{1,2,0:T(8,128)}, u32[]{:S(2)}, u32[]{:S(2)}) async-start(f32[32,500,576]{1,2,0:T(8,128)} %copy.77), calls=%async_computation.4 | async-start | bytes 75497472 | tf_op jit(solution)/shard_map/all_to_all | solution.py:41
  3356.8 60.8 %copy-start.14 = (pred[32,750]{1,0:T(8,128)(4,1)S(1)}, pred[32,750]{1,0:T(8,128)(4,1)}, u32[]{:S(2)}) copy-start(pred[32,750]{1,0:T(8,128)(4,1)} %broadcast_in_dim.123) | copy-start | bytes 72004
  3495.2 524.0 %copy-start.10 = (s32[32,1,500]{2,1,0:T(1,128)S(1)}, s32[32,1,500]{2,1,0:T(1,128)}, u32[]{:S(2)}) copy-start(s32[32,1,500]{2,1,0:T(1,128)} %copy-done.9) | copy-start | bytes 192004
  3495.2 524.3 %copy-start.13 = (s32[32,750]{1,0:T(8,128)S(1)}, s32[32,750]{1,0:T(8,128)}, u32[]{:S(2)}) copy-start(s32[32,750]{1,0:T(8,128)} %get-tuple-element.62) | copy-start | bytes 288004
  3983.8 1256.2 %all-to-all-start.5 = ((f32[32,750,576]{1,2,0:T(8,128)}), f32[32,750,576]{1,2,0:T(8,128)}, u32[]{:S(2)}, u32[]{:S(2)}) async-start(f32[32,750,576]{1,2,0:T(8,128)} %copy.83), calls=%async_computation.5 | async-start | bytes 113246208 | tf_op jit(solution)/shard_map/all_to_all | solution.py:41
  (8 other events, 82.7 us)
where the time goes:
time: 5600 us; the launch traced here: 5530 us
  waiting for transfers between devices  3110 us (56%)
  local copies, waits for them, and re-layouts  1650 us (29%)
  other arithmetic  574 us (10%)
  starting transfers between devices  141 us (3%)
  matrix products  58.6 us (1%)
    all_to_all x2, waiting for transfers between devices, fetch_rows(): returned = lax.all_to_all(rows_found, AXIS_NAME, 0, 0)  1600 us
    all_to_all x2, waiting for transfers between devices, send_grads(): lax.all_to_all(grad_cells.reshape(shards, capacity, -1), AXIS_NAME, 0, 0)  1510 us
    gather x6, local copies, waits for them, and re-layouts, fetch_rows(): rows_found = jnp.take(table_shard, local_rows, axis=0)  324 us
    scatter-add x2, other arithmetic, send_grads(): jax.ops.segment_sum(arrived.reshape(shards * capacity, -1), local_rows, n...  281 us
    gather x2, local copies, waits for them, and re-layouts, send_layout(): jnp.take(id_list, slot_of_cell, axis=0, mode='fill', fill_value=-1)  206 us
    gather x3, local copies, waits for them, and re-layouts, device_step(): jnp.take(jnp.concatenate([d_context, d_negative]), out_slot, axis=0, mode...  200 us
    reshape x4, local copies, waits for them, and re-layouts, fetch_rows(): returned.reshape(shards * capacity, table_shard.shape[1])  184 us
    reshape x4, local copies, waits for them, and re-layouts, send_grads(): arrived.reshape(shards * capacity, -1)  184 us
  transfers between devices with their start and end apart: 6, of which 4 were waited for; matrix products, arithmetic and copies ran while one was open for 25% of the time, Pallas kernels for 0%

commit v1 on v0

v1 whole, which is shorter than its diff:
```python
import jax
import jax.numpy as jnp
from jax import lax
from jax.sharding import PartitionSpec as P


LEARN_RATE = 1.0
NEG_WEIGHT = 5.0
AXIS_NAME = 'vp'
PLANE = 8
POS_BITS = 13
CELL_BITS = 14
NO_KEY = 2 ** 30
LANES = 128


def distinct_capacity(num_ids, shards):
    common_slots = 3 * num_ids // shards
    return common_slots // 4 + (num_ids - common_slots + shards - 1) // shards


def plan_list(id_list, shard_rows, lines, capacity):
    num_ids = id_list.shape[0]
    column_rows = lines * shard_rows
    shard_idx = id_list // shard_rows
    peer = shard_idx % PLANE
    row_key = peer * column_rows + (shard_idx // PLANE) * shard_rows + id_list % shard_rows
    packed = lax.sort((row_key << POS_BITS) | jnp.arange(num_ids, dtype=jnp.int32), is_stable=False)
    key_sorted = packed >> POS_BITS
    slot_sorted = packed & (2 ** POS_BITS - 1)
    is_first = jnp.concatenate([jnp.ones((1,), bool), key_sorted[1:] != key_sorted[:-1]])
    rank = jnp.cumsum(is_first.astype(jnp.int32)) - 1
    peer_sorted = key_sorted // column_rows
    below = (peer_sorted[None, :] < jnp.arange(PLANE + 1, dtype=jnp.int32)[:, None]) & is_first[None, :]
    start = jnp.sum(below.astype(jnp.int32), axis=1)
    start_sorted = jnp.sum(jnp.where(peer_sorted[None, :] == jnp.arange(PLANE, dtype=jnp.int32)[:, None], start[:PLANE, None], 0), axis=0)
    cell_sorted = peer_sorted * capacity + rank - start_sorted
    cell_of_id = lax.sort((slot_sorted << CELL_BITS) | cell_sorted, is_stable=False) & (2 ** CELL_BITS - 1)
    distinct = jnp.pad(lax.sort(jnp.where(is_first, key_sorted, NO_KEY), is_stable=False), (0, capacity))
    place = jnp.arange(capacity, dtype=jnp.int32)
    asks = []
    for p in range(PLANE):
        row = lax.dynamic_slice(distinct, (start[p],), (capacity,)) - p * column_rows
        asks.append(jnp.where(place < start[p + 1] - start[p], row, place))
    return cell_of_id, jnp.stack(asks)


def pair_grads(center_vec, context_vec, negative_vec):
    neg_scale = NEG_WEIGHT / negative_vec.shape[0]
    pos_score = jnp.sum(center_vec * context_vec, axis=1)
    center_half = center_vec.astype(jnp.bfloat16)
    negative_half = negative_vec.astype(jnp.bfloat16)
    neg_score = lax.dot_general(center_half, negative_half, (((1,), (1,)), ((), ())), preferred_element_type=jnp.float32)
    pos_grad = (jax.nn.sigmoid(pos_score) - 1.0)[:, None]
    neg_grad = (neg_scale * jax.nn.sigmoid(neg_score)).astype(jnp.bfloat16)
    d_center = pos_grad * context_vec + jnp.dot(neg_grad, negative_half, preferred_element_type=jnp.float32)
    d_context = pos_grad * center_vec
    d_negative = lax.dot_general(neg_grad, center_half, (((0,), (0,)), ((), ())), preferred_element_type=jnp.float32)
    return d_center, d_context, d_negative


def widen(shard, width):
    return jnp.pad(shard, ((0, 0), (0, width - shard.shape[1])))


def take_rows(table, rows):
    return table.at[rows].get(mode='promise_in_bounds')


def add_rows(num_rows, rows, values):
    return jnp.zeros((num_rows, values.shape[1]), values.dtype).at[rows].add(values, mode='promise_in_bounds')


def solution(mesh):
    shards = mesh.shape[AXIS_NAME]
    lines = shards // PLANE
    plane_groups = [[line * PLANE + q for q in range(PLANE)] for line in range(lines)]
    line_groups = [[line * PLANE + q for line in range(lines)] for q in range(PLANE)]

    def exchange(cells):
        return lax.all_to_all(cells, AXIS_NAME, 0, 0, axis_index_groups=plane_groups)

    def gather_lines(shard):
        return lax.all_gather(shard, AXIS_NAME, axis_index_groups=line_groups, tiled=True)

    def sum_lines(column):
        return lax.psum_scatter(column, AXIS_NAME, scatter_dimension=0, axis_index_groups=line_groups, tiled=True)

    def device_step(in_shard, out_shard, center_ids, context_ids, negative_ids):
        shard_rows, dim = in_shard.shape
        wide = -(-dim // LANES) * LANES
        pairs_dev = center_ids.shape[0]
        column_rows = lines * shard_rows
        cap_in = lines * distinct_capacity(pairs_dev, shards)
        cap_out = cap_in + lines * distinct_capacity(negative_ids.shape[0], shards)
        out_column = gather_lines(widen(out_shard, wide))
        out_cell, out_asks = plan_list(jnp.concatenate([context_ids, negative_ids]), shard_rows, lines, cap_out)
        in_column = gather_lines(widen(in_shard, wide))
        in_cell, in_asks = plan_list(center_ids, shard_rows, lines, cap_in)
        asked = exchange(jnp.concatenate([out_asks, in_asks], axis=1))
        out_asked = asked[:, :cap_out].reshape(-1)
        in_asked = asked[:, cap_out:].reshape(-1)
        out_found = take_rows(out_column, out_asked).reshape(PLANE, cap_out, wide)
        out_rows = exchange(out_found).reshape(-1, wide)
        in_found = take_rows(in_column, in_asked).reshape(PLANE, cap_in, wide)
        in_rows = exchange(in_found).reshape(-1, wide)
        looked_up = take_rows(out_rows, out_cell)
        center_vec = take_rows(in_rows, in_cell)
        d_center, d_context, d_negative = pair_grads(center_vec, looked_up[:pairs_dev], looked_up[pairs_dev:])
        in_cells = add_rows(PLANE * cap_in, in_cell, d_center)
        in_back = exchange(in_cells.reshape(PLANE, cap_in, wide)).reshape(-1, wide)
        out_cells = add_rows(PLANE * cap_out, out_cell, jnp.concatenate([d_context, d_negative]))
        out_back = exchange(out_cells.reshape(PLANE, cap_out, wide)).reshape(-1, wide)
        in_sum = sum_lines(add_rows(column_rows, in_asked, in_back))
        out_sum = sum_lines(add_rows(column_rows, out_asked, out_back))
        return in_shard - LEARN_RATE * in_sum[:, :dim], out_shard - LEARN_RATE * out_sum[:, :dim]

    return jax.shard_map(device_step, mesh=mesh, in_specs=(P(AXIS_NAME, None), P(AXIS_NAME, None), P(AXIS_NAME), P(AXIS_NAME), P(AXIS_NAME)), out_specs=(P(AXIS_NAME, None), P(AXIS_NAME, None)), check_vma=False)
```

time: 5600 us -> 2020 us (0.36)
  waiting for transfers between devices: 3110 us -> 909 us
  local copies, waits for them, and re-layouts: 1650 us -> 174 us
  blocking collectives: 0 us -> 500 us
  other arithmetic: 574 us -> 281 us
  starting transfers between devices: 141 us -> 12.6 us
  between operations: 1.69 us -> 63.6 us
    all_to_all x6 -> x2, waiting for transfers between devices: 3110 us -> 246 us  [exchange(): lax.all_to_all(cells, AXIS_NAME, 0, 0, axis_index_groups=plane_groups)]
    gather x24 -> x4, local copies, waits for them, and re-layouts: 1020 us -> 141 us  [take_rows(): return table.at[rows].get(mode='promise_in_bounds')]
    all_to_all x0 -> x3, blocking collectives: none -> 500 us  [exchange(): lax.all_to_all(cells, AXIS_NAME, 0, 0, axis_index_groups=plane_groups)]
    all_gather x0 -> x2, waiting for transfers between devices: none -> 411 us  [gather_lines(): lax.all_gather(shard, AXIS_NAME, axis_index_groups=line_groups, tiled=True)]
    reshape x8 -> x2, local copies, waits for them, and re-layouts: 368 us -> 0.24 us  [the longest x1 0.13 us: device_step(): out_asked = asked[:, :cap_out].reshape(-1)]
    reduce_scatter x0 -> x2, waiting for transfers between devices: none -> 251 us  [sum_lines(): lax.psum_scatter(column, AXIS_NAME, scatter_dimension=0, axis_index_group...]
    scatter-add x4, other arithmetic: 353 us -> 216 us  [add_rows(): jnp.zeros((num_rows, values.shape[1]), values.dtype).at[rows]]
    all_to_all x6 -> x2, starting transfers between devices: 141 us -> 12.2 us  [exchange(): lax.all_to_all(cells, AXIS_NAME, 0, 0, axis_index_groups=plane_groups)]
  transfers between devices with their start and end apart: 6 -> 6, of which waited for: 4 -> 4; matrix products, arithmetic and copies ran while one was open for 25% -> 16% of each run, Pallas kernels for 0% -> 0%
where the time goes in v1:
time: 2020 us; the launch traced here: 2000 us
  waiting for transfers between devices  909 us (45%)
  blocking collectives  500 us (25%)
  other arithmetic  281 us (14%)
  local copies, waits for them, and re-layouts  174 us (9%)
  matrix products  64.7 us (3%)
  between operations  63.6 us (3%)
    all_to_all x3, blocking collectives, exchange(): lax.all_to_all(cells, AXIS_NAME, 0, 0, axis_index_groups=plane_groups)  500 us
    all_gather x2, waiting for transfers between devices, gather_lines(): lax.all_gather(shard, AXIS_NAME, axis_index_groups=line_groups, tiled=True)  411 us
    reduce_scatter x2, waiting for transfers between devices, sum_lines(): lax.psum_scatter(column, AXIS_NAME, scatter_dimension=0, axis_index_group...  251 us
    all_to_all x2, waiting for transfers between devices, exchange(): lax.all_to_all(cells, AXIS_NAME, 0, 0, axis_index_groups=plane_groups)  246 us
    scatter-add x4, other arithmetic, add_rows(): jnp.zeros((num_rows, values.shape[1]), values.dtype).at[rows]  216 us
    gather x4, local copies, waits for them, and re-layouts, take_rows(): return table.at[rows].get(mode='promise_in_bounds')  141 us
  transfers between devices with their start and end apart: 6, of which 4 were waited for; matrix products, arithmetic and copies ran while one was open for 16% of the time, Pallas kernels for 0%

profile of v1, /device:TPU:24, one launch (start us, length us, event | category | flops | bytes accessed | tf_op | source)
XLA Modules:
  0.0 2004.0 jit_solution(12453678813751200472)
XLA Ops:
  100.9 8.6 all_to_all.32
  110.4 176.3 %all-gather.3.cloned.1.call-done = f32[6144,640]{1,0:T(8,128)} async-done(((f32[1536,640]{1,0:T(8,128)}), f32[6144,640]{1,0:T(8,128)}) %all-gather.3.cloned.1.call-update) | async-done | bytes 15728656 | tf_op jit(solution)/shard_map/all_gather | solution.py:84
  286.7 28.4 %gather_fusion = f32[6784,640]{1,0:T(8,128)} fusion(f32[6144,640]{1,0:T(8,128)} %all-gather.3.cloned.1.call-done, s32[7168]{0:T(1024)S(1)} %pad_clamp_fusion.1), kind=kCustom, calls=%fused_computation | custom fusion | bytes 34761216 | tf_op jit(solution)/shard_map/gather | solution.py:67
  315.1 5.8 all-to-all-start.1
  321.8 234.7 %all-gather.5.cloned.1.call-done = f32[6144,640]{1,0:T(8,128)} async-done(((f32[1536,640]{1,0:T(8,128)}), f32[6144,640]{1,0:T(8,128)}) %all-gather.5.cloned.1.call-update) | async-done | bytes 15728656 | tf_op jit(solution)/shard_map/all_gather | solution.py:84
  556.5 51.1 %gather_fusion.2 = f32[10176,640]{1,0:T(8,128)} fusion(f32[6144,640]{1,0:T(8,128)} %all-gather.5.cloned.1.call-done, s32[10240]{0:T(1024)S(1)} %pad_clamp_fusion), kind=kCustom, calls=%fused_computation.2 | custom fusion | bytes 52141824 | tf_op jit(solution)/shard_map/gather | solution.py:67
  607.6 6.5 all-to-all-start.2
  626.0 24.9 %gather_fusion.1 = f32[4096,640]{1,0:T(8,128)} fusion(f32[6784,640]{1,0:T(8,128)} %bitcast.21, s32[4096]{0:T(1024)S(1)} %get-tuple-element.22), kind=kCustom, calls=%fused_computation.1 | custom fusion | bytes 20987904 | tf_op jit(solution)/shard_map/gather | solution.py:67
  650.9 246.5 %all-to-all-done.2 = f32[8,1272,640]{2,1,0:T(8,128)} async-done(((f32[8,1272,640]{2,1,0:T(8,128)}), f32[8,1272,640]{2,1,0:T(8,128)}, u32[]{:S(2)}, u32[]{:S(2)}) %all-to-all-start.2) | async-done | bytes 26050592 | tf_op jit(solution)/shard_map/all_to_all | solution.py:81
  897.4 36.2 %gather_fusion.3 = f32[6144,640]{1,0:T(8,128)} fusion(f32[10176,640]{1,0:T(8,128)} %bitcast.24, s32[6144]{0:T(1024)S(1)} %get-tuple-element.9), kind=kCustom, calls=%fused_computation.3 | custom fusion | bytes 31481856 | tf_op jit(solution)/shard_map/gather | solution.py:67
  933.6 7.9 multiply_reduce_fusion
  941.5 24.4 %multiply_convert_fusion = bf16[4096,2048]{1,0:T(8,128)(2,1)} fusion(f32[4096,640]{1,0:T(8,128)} %gather_fusion.1, f32[6144,640]{1,0:T(8,128)} %gather_fusion.3), kind=kOutput, calls=%fused_computation.8 | convolution fusion | flops 10781982720 | bytes 29884416 | tf_op jit(solution)/shard_map/dot_general | solution.py:53
  966.0 19.9 fusion.18
  985.9 37.0 %scatter_custom_fusion = f32[6784,640]{1,0:T(8,128)} fusion(s32[4096]{0:T(1024)} %get-tuple-element.23, f32[4096,640]{1,0:T(8,128)} %fusion.18, f32[6144,640]{1,0:T(8,128)} %gather_fusion.3, f32[]{:T(128)} %constant.138.clone.1, f32[4096]{0:T(1024)S(1)} %divide_add_fusion), kind=kCustom, calls=%fused_computation.14 | custom fusion | flops 7864320 | bytes 38355456 | tf_op jit(solution)/shard_map/scatter-add | solution.py:71
  1022.9 198.4 %all_to_all.33 = f32[8,848,640]{2,1,0:T(8,128)} all-to-all(f32[8,848,640]{2,1,0:T(8,128)} %bitcast.53), channel_id=1, replica_groups={{0,1,2,3,4,5,6,7},{8,9,10,11,12,13,14,15},{16,17,18,19,20,21,22,23},{24..., dimensions={0} | all-to-all | bytes 34734080 | tf_op jit(solution)/shard_map/all_to_all | solution.py:81
  1221.3 53.4 %scatter_custom_fusion.1 = f32[6144,640]{1,0:T(8,128)} fusion(s32[6784]{0:T(1024)} %copy-done.2, f32[6784,640]{1,0:T(8,128)} %bitcast.55, f32[]{:T(128)} %constant.138.clone.1), kind=kCustom, calls=%fused_computation.22 | custom fusion | flops 4341760 | bytes 15729152 | tf_op jit(solution)/shard_map/scatter-add | solution.py:71
  1274.8 9.7 broadcast_multiply_fusion
  1284.4 20.4 %fusion.15 = f32[2048,640]{1,0:T(8,128)} fusion(bf16[4096,2048]{1,0:T(8,128)(2,1)} %multiply_convert_fusion, f32[4096,640]{1,0:T(8,128)} %gather_fusion.1), kind=kOutput, calls=%fused_computation.29 | convolution fusion | flops 10740039680 | bytes 32505856 | tf_op jit(solution)/shard_map/dot_general | solution.py:58
  1304.8 52.9 %scatter_custom_fusion.2 = f32[10176,640]{1,0:T(8,128)} fusion(s32[6144]{0:T(1024)} %get-tuple-element.8, f32[2048,640]{1,0:T(8,128)} %fusion.15, f32[]{:T(128)} %constant.180, f32[4096,640]{1,0:T(8,128)} %broadcast_multiply_fusion, f32[]{:T(128)} %constant.138.clone.1), kind=kCustom, calls=%fused_computation.9 | custom fusion | flops 7864320 | bytes 41780224 | tf_op jit(solution)/shard_map/scatter-add | solution.py:71
  1357.7 293.1 %all_to_all.34 = f32[8,1272,640]{2,1,0:T(8,128)} all-to-all(f32[8,1272,640]{2,1,0:T(8,128)} %bitcast.50), channel_id=1, replica_groups={{0,1,2,3,4,5,6,7},{8,9,10,11,12,13,14,15},{16,17,18,19,20,21,22,23},{24..., dimensions={0} | all-to-all | bytes 52101120 | tf_op jit(solution)/shard_map/all_to_all | solution.py:81
  1650.9 73.0 %scatter_custom_fusion.3 = f32[6144,640]{1,0:T(8,128)} fusion(s32[10176]{0:T(1024)} %bitcast.59, f32[10176,640]{1,0:T(8,128)} %bitcast.54, f32[]{:T(128)} %constant.138.clone.1), kind=kCustom, calls=%fused_computation.20 | custom fusion | flops 6512640 | bytes 15729152 | tf_op jit(solution)/shard_map/scatter-add | solution.py:71
  1723.9 5.8 slice_subtract_fusion.1
  1735.2 251.1 %reduce-scatter.5.cloned.1.call-done = f32[1536,640]{1,0:T(8,128)} async-done(((f32[6144,640]{1,0:T(8,128)}), f32[1536,640]{1,0:T(8,128)}) %reduce-scatter.5.cloned.1.call-update) | async-done | bytes 3932176 | tf_op jit(solution)/shard_map/reduce_scatter | solution.py:87
  1986.3 5.6 slice_subtract_fusion
  (92 shorter events, 68.7 us)
Async XLA Ops:
  7.2 9.9 copy-start
  7.2 279.5 %all-gather.3.cloned.1.call-start = ((), (), s32[]{:S(2)}) async-start(), calls=%async_computation.7 | async-start | bytes 19660800 | tf_op jit(solution)/shard_map/all_gather | solution.py:84
  12.7 11.8 copy-start.3
  17.0 539.5 %all-gather.5.cloned.1.call-start = ((), (), s32[]{:S(2)}) async-start(), calls=%async_computation.8 | async-start | bytes 19660800 | tf_op jit(solution)/shard_map/all_gather | solution.py:84
  109.8 0.6 copy-start.2
  315.1 292.5 %all-to-all-start.1 = ((f32[8,848,640]{2,1,0:T(8,128)}), f32[8,848,640]{2,1,0:T(8,128)}, u32[]{:S(2)}, u32[]{:S(2)}) async-start(f32[8,848,640]{2,1,0:T(8,128)} %bitcast.52), calls=%async_computation.1 | async-start | bytes 34734080 | tf_op jit(solution)/shard_map/all_to_all | solution.py:81
  321.1 0.6 copy-start.1
  607.6 289.8 %all-to-all-start.2 = ((f32[8,1272,640]{2,1,0:T(8,128)}), f32[8,1272,640]{2,1,0:T(8,128)}, u32[]{:S(2)}, u32[]{:S(2)}) async-start(f32[8,1272,640]{2,1,0:T(8,128)} %bitcast.51), calls=%async_computation.2 | async-start | bytes 52101120 | tf_op jit(solution)/shard_map/all_to_all | solution.py:81
  614.1 1109.8 %reduce-scatter.3.cloned.1.call-start = ((), (), s32[]{:S(2)}) async-start(), calls=%async_computation.9 | async-start | bytes 19660800 | tf_op jit(solution)/shard_map/reduce_scatter | solution.py:87
  1274.7 711.6 %reduce-scatter.5.cloned.1.call-start = ((), (), s32[]{:S(2)}) async-start(), calls=%async_computation.10 | async-start | bytes 19660800 | tf_op jit(solution)/shard_map/reduce_scatter | solution.py:87
Sparse Core Ops, SparseCore 0:
  17.1 269.5 all-gather.2
  288.3 268.1 all-gather.4
  1274.9 261.8 reduce-scatter.2
  1724.0 262.2 reduce-scatter.4

commit v2 on v1

v2 whole, which is shorter than its diff:
```python
import functools

import jax
import jax.numpy as jnp
from jax import lax
from jax.experimental import pallas as pl
from jax.experimental.pallas import tpu as pltpu
from jax.sharding import PartitionSpec as P


LEARN_RATE = 1.0
NEG_WEIGHT = 5.0
AXIS_NAME = 'vp'
PLANE = 8
POS_BITS = 13
CELL_BITS = 14
NO_KEY = 2 ** 30
LANES = 128
CUTS = (0, 128, 384)
CHUNKS = range(len(CUTS))
PAIR_BLOCK = 512


def distinct_capacity(num_ids, shards):
    common_slots = 3 * num_ids // shards
    return common_slots // 4 + (num_ids - common_slots + shards - 1) // shards


def plan_list(id_list, shard_rows, lines, capacity):
    num_ids = id_list.shape[0]
    column_rows = lines * shard_rows
    shard_idx = id_list // shard_rows
    peer = shard_idx % PLANE
    row_key = peer * column_rows + (shard_idx // PLANE) * shard_rows + id_list % shard_rows
    packed = lax.sort((row_key << POS_BITS) | jnp.arange(num_ids, dtype=jnp.int32), is_stable=False)
    key_sorted = packed >> POS_BITS
    slot_sorted = packed & (2 ** POS_BITS - 1)
    is_first = jnp.concatenate([jnp.ones((1,), bool), key_sorted[1:] != key_sorted[:-1]])
    rank = jnp.cumsum(is_first.astype(jnp.int32)) - 1
    peer_sorted = key_sorted // column_rows
    below = (peer_sorted[None, :] < jnp.arange(PLANE + 1, dtype=jnp.int32)[:, None]) & is_first[None, :]
    start = jnp.sum(below.astype(jnp.int32), axis=1)
    start_sorted = jnp.sum(jnp.where(peer_sorted[None, :] == jnp.arange(PLANE, dtype=jnp.int32)[:, None], start[:PLANE, None], 0), axis=0)
    cell_sorted = peer_sorted * capacity + rank - start_sorted
    cell_of_id = lax.sort((slot_sorted << CELL_BITS) | cell_sorted, is_stable=False) & (2 ** CELL_BITS - 1)
    distinct = jnp.pad(lax.sort(jnp.where(is_first, key_sorted, NO_KEY), is_stable=False), (0, capacity))
    place = jnp.arange(capacity, dtype=jnp.int32)
    asks = []
    for p in range(PLANE):
        row = lax.dynamic_slice(distinct, (start[p],), (capacity,)) - p * column_rows
        asks.append(jnp.where(place < start[p + 1] - start[p], row, place))
    return cell_of_id, jnp.stack(asks)


def pair_kernel(neg_scale, bounds, *refs):
    n = len(bounds)
    center, context, negative, d_center, d_context, d_negative = (refs[k * n:(k + 1) * n] for k in range(6))
    neg_half = refs[6 * n]

    @pl.when(pl.program_id(0) == 0)
    def _():
        for k, (lo, hi) in enumerate(bounds):
            neg_half[:, lo:hi] = negative[k][...].astype(jnp.bfloat16)
            d_negative[k][...] = jnp.zeros_like(d_negative[k])

    u = [r[...] for r in center]
    v = [r[...] for r in context]
    pos_score = sum(jnp.sum(a * b, axis=1, keepdims=True) for a, b in zip(u, v))
    pos_grad = jax.nn.sigmoid(pos_score) - 1.0
    center_half = jnp.concatenate([a.astype(jnp.bfloat16) for a in u], axis=1)
    neg_score = lax.dot_general(center_half, neg_half[...], (((1,), (1,)), ((), ())), preferred_element_type=jnp.float32)
    neg_grad = (neg_scale * jax.nn.sigmoid(neg_score)).astype(jnp.bfloat16)
    from_neg = jnp.dot(neg_grad, neg_half[...], preferred_element_type=jnp.float32)
    to_neg = lax.dot_general(neg_grad, center_half, (((0,), (0,)), ((), ())), preferred_element_type=jnp.float32)
    for k, (lo, hi) in enumerate(bounds):
        d_context[k][...] = pos_grad * u[k]
        d_center[k][...] = pos_grad * v[k] + from_neg[:, lo:hi]
        d_negative[k][...] += to_neg[:, lo:hi]


def pair_grads(center, looked_up):
    pairs, negs = center[0].shape[0], looked_up[0].shape[0] - center[0].shape[0]
    widths = [c.shape[1] for c in center]
    total, n = sum(widths), len(widths)
    bounds = [(sum(widths[:k]), sum(widths[:k + 1])) for k in range(n)]
    pair_specs = [pl.BlockSpec((PAIR_BLOCK, w), lambda i: (i, 0)) for w in widths]
    neg_in_specs = [pl.BlockSpec((negs, w), lambda i: (pairs // negs, 0)) for w in widths]
    neg_out_specs = [pl.BlockSpec((negs, w), lambda i: (0, 0)) for w in widths]
    shapes = [jax.ShapeDtypeStruct((m, w), jnp.float32) for m in (pairs, pairs, negs) for w in widths]
    grads = pl.pallas_call(
        functools.partial(pair_kernel, NEG_WEIGHT / negs, bounds),
        grid=(pairs // PAIR_BLOCK,),
        in_specs=pair_specs + pair_specs + neg_in_specs,
        out_specs=pair_specs + pair_specs + neg_out_specs,
        out_shape=shapes,
        scratch_shapes=[pltpu.VMEM((negs, total), jnp.bfloat16)],
        compiler_params=pltpu.CompilerParams(dimension_semantics=('arbitrary',), vmem_limit_bytes=60 * 2 ** 20),
        cost_estimate=pl.CostEstimate(flops=6 * pairs * negs * total, bytes_accessed=4 * total * (4 * pairs + 2 * negs), transcendentals=2 * pairs * negs),
    )(*center, *looked_up, *looked_up)
    return grads[:n], grads[n:2 * n], grads[2 * n:]


def column_chunks(shard):
    parts = [shard[:, lo:hi] for lo, hi in zip(CUTS, CUTS[1:] + (shard.shape[1],))]
    return [jnp.pad(x, ((0, 0), (0, -x.shape[1] % LANES))) for x in parts]


def take_rows(table, rows):
    return table.at[rows].get(mode='promise_in_bounds')


def add_rows(num_rows, *parts):
    total = jnp.zeros((num_rows, parts[0][1].shape[1]), parts[0][1].dtype)
    for rows, values in parts:
        total = total.at[rows].add(values, mode='promise_in_bounds')
    return total


FETCH_ORDER = [('out', k) for k in CHUNKS] + [('in', k) for k in reversed(CHUNKS)]
BACK_ORDER = FETCH_ORDER[::-1]


def solution(mesh):
    shards = mesh.shape[AXIS_NAME]
    lines = shards // PLANE
    plane_groups = [[line * PLANE + q for q in range(PLANE)] for line in range(lines)]
    line_groups = [[line * PLANE + q for line in range(lines)] for q in range(PLANE)]

    def exchange(cells):
        return lax.all_to_all(cells, AXIS_NAME, 0, 0, axis_index_groups=plane_groups)

    def gather_lines(shard):
        return lax.all_gather(shard, AXIS_NAME, axis_index_groups=line_groups, tiled=True)

    def sum_lines(column):
        return lax.psum_scatter(column, AXIS_NAME, scatter_dimension=0, axis_index_groups=line_groups, tiled=True)

    def device_step(in_shard, out_shard, center_ids, context_ids, negative_ids):
        shard_rows, dim = in_shard.shape
        pairs_dev = center_ids.shape[0]
        num_rows = lines * shard_rows
        cap_in = lines * distinct_capacity(pairs_dev, shards)
        cap_out = cap_in + lines * distinct_capacity(negative_ids.shape[0], shards)
        capacity = {'out': cap_out, 'in': cap_in}
        shard = {'out': column_chunks(out_shard), 'in': column_chunks(in_shard)}
        column = {}
        for side, k in FETCH_ORDER:
            column[side, k] = gather_lines(shard[side][k])
        out_cell, out_asks = plan_list(jnp.concatenate([context_ids, negative_ids]), shard_rows, lines, cap_out)
        in_cell, in_asks = plan_list(center_ids, shard_rows, lines, cap_in)
        asked_all = exchange(jnp.concatenate([out_asks, in_asks], axis=1))
        asked = {'out': asked_all[:, :cap_out].reshape(-1), 'in': asked_all[:, cap_out:].reshape(-1)}
        cell = {'out': out_cell, 'in': in_cell}
        looked_up = {}
        for side, k in FETCH_ORDER:
            found = take_rows(column[side, k], asked[side]).reshape(PLANE, capacity[side], -1)
            returned = exchange(found)
            looked_up[side, k] = take_rows(returned.reshape(-1, returned.shape[2]), cell[side])
        d_center, d_context, d_negative = pair_grads([looked_up['in', k] for k in CHUNKS], [looked_up['out', k] for k in CHUNKS])
        row_sum = {}
        for side, k in BACK_ORDER:
            parts = [(in_cell, d_center[k])] if side == 'in' else [(out_cell[:pairs_dev], d_context[k]), (out_cell[pairs_dev:], d_negative[k])]
            cells = add_rows(PLANE * capacity[side], *parts)
            arrived = exchange(cells.reshape(PLANE, capacity[side], -1))
            dense = add_rows(num_rows, (asked[side], arrived.reshape(-1, arrived.shape[2])))
            row_sum[side, k] = sum_lines(dense)
        new = []
        for side, old in (('in', in_shard), ('out', out_shard)):
            grad = jnp.concatenate([row_sum[side, k] for k in CHUNKS], axis=1)[:, :dim]
            new.append(old - LEARN_RATE * grad)
        return tuple(new)

    return jax.shard_map(device_step, mesh=mesh, in_specs=(P(AXIS_NAME, None), P(AXIS_NAME, None), P(AXIS_NAME), P(AXIS_NAME), P(AXIS_NAME)), out_specs=(P(AXIS_NAME, None), P(AXIS_NAME, None)), check_vma=False)
```

time: 2020 us -> 1900 us (0.941)
  waiting for transfers between devices: 909 us -> 502 us
  other arithmetic: 281 us -> 540 us
  local copies, waits for them, and re-layouts: 174 us -> 347 us
  blocking collectives: 500 us -> 344 us
  matrix products: 64.7 us -> 0 us
  Pallas kernels: 0 us -> 48.1 us
  starting transfers between devices: 12.6 us -> 39.9 us
    scatter-add x4 -> x15, other arithmetic: 216 us -> 491 us  [add_rows(): total = total.at[rows].add(values, mode='promise_in_bounds')]
    all_to_all x2 -> x8, waiting for transfers between devices: 246 us -> 78 us  [exchange(): lax.all_to_all(cells, AXIS_NAME, 0, 0, axis_index_groups=plane_groups)]
    gather x4 -> x12, local copies, waits for them, and re-layouts: 141 us -> 306 us  [take_rows(): return table.at[rows].get(mode='promise_in_bounds')]
    all_to_all x3 -> x5, blocking collectives: 500 us -> 344 us  [exchange(): lax.all_to_all(cells, AXIS_NAME, 0, 0, axis_index_groups=plane_groups)]
    reduce_scatter x2 -> x6, waiting for transfers between devices: 251 us -> 98.4 us  [sum_lines(): lax.psum_scatter(column, AXIS_NAME, scatter_dimension=0, axis_index_group...]
    all_gather x2 -> x6, waiting for transfers between devices: 411 us -> 325 us  [gather_lines(): lax.all_gather(shard, AXIS_NAME, axis_index_groups=line_groups, tiled=True)]
    dot_general x3 -> x0, matrix products: 64.7 us -> none  [the longest x1 24.4 us: pair_grads(): lax.dot_general(center_half, negative_half, (((1,), (1,)), ((), ())), pre...]
    pallas_call x0 -> x1, Pallas kernels: none -> 48.1 us  [pair_grads(): pl.pallas_call(functools.partial(pair_kernel, NEG_WEIGHT / negs, bounds),...]
  transfers between devices with their start and end apart: 6 -> 20, of which waited for: 4 -> 10; matrix products, arithmetic and copies ran while one was open for 16% -> 41% of each run, Pallas kernels for 0% -> 0%
where the time goes in v2:
time: 1900 us; the launch traced here: 1890 us
  other arithmetic  540 us (28%)
  waiting for transfers between devices  502 us (26%)
  local copies, waits for them, and re-layouts  347 us (18%)
  blocking collectives  344 us (18%)
  between operations  64.7 us (3%)
  Pallas kernels  48.1 us (3%)
  starting transfers between devices  39.9 us (2%)
    scatter-add x15, other arithmetic, add_rows(): total = total.at[rows].add(values, mode='promise_in_bounds')  491 us
    all_to_all x5, blocking collectives, exchange(): lax.all_to_all(cells, AXIS_NAME, 0, 0, axis_index_groups=plane_groups)  344 us
    all_gather x6, waiting for transfers between devices, gather_lines(): lax.all_gather(shard, AXIS_NAME, axis_index_groups=line_groups, tiled=True)  325 us
    gather x12, local copies, waits for them, and re-layouts, take_rows(): return table.at[rows].get(mode='promise_in_bounds')  306 us
    reduce_scatter x6, waiting for transfers between devices, sum_lines(): lax.psum_scatter(column, AXIS_NAME, scatter_dimension=0, axis_index_group...  98.4 us
    all_to_all x8, waiting for transfers between devices, exchange(): lax.all_to_all(cells, AXIS_NAME, 0, 0, axis_index_groups=plane_groups)  78 us
    pallas_call x1, Pallas kernels, pair_grads(): pl.pallas_call(functools.partial(pair_kernel, NEG_WEIGHT / negs, bounds),...  48.1 us
    all_to_all x8, starting transfers between devices, exchange(): lax.all_to_all(cells, AXIS_NAME, 0, 0, axis_index_groups=plane_groups)  39 us
  transfers between devices with their start and end apart: 20, of which 10 were waited for; matrix products, arithmetic and copies ran while one was open for 41% of the time, Pallas kernels for 0%

profile of v2, /device:TPU:24, one launch (start us, length us, event | category | flops | bytes accessed | tf_op | source)
XLA Modules:
  0.0 1885.1 jit_solution(18146930692689547597)
XLA Ops:
  142.0 36.2 %gather_fusion.6 = f32[10176,128]{1,0:T(8,128)} fusion(f32[6144,128]{1,0:T(8,128)} %all-gather.13.cloned.1.call-done, s32[10240]{0:T(1024)S(1)} %pad_clamp_fusion), kind=kCustom, calls=%fused_computation.6 | custom fusion | bytes 10460928 | tf_op jit(solution)/shard_map/gather | solution.py:109
  182.9 74.3 %all-gather.11.cloned.1.call-done = f32[6144,256]{1,0:T(8,128)} async-done(((f32[1536,256]{1,0:T(8,128)}), f32[6144,256]{1,0:T(8,128)}) %all-gather.11.cloned.1.call-update) | async-done | bytes 6291472 | tf_op jit(solution)/shard_map/all_gather | solution.py:133
  284.7 88.1 %all-gather.9.cloned.1.call-done = f32[6144,256]{1,0:T(8,128)} async-done(((f32[1536,256]{1,0:T(8,128)}), f32[6144,256]{1,0:T(8,128)}) %all-gather.9.cloned.1.call-update) | async-done | bytes 6291472 | tf_op jit(solution)/shard_map/all_gather | solution.py:133
  400.4 87.9 %all-gather.15.cloned.1.call-done = f32[6144,256]{1,0:T(8,128)} async-done(((f32[1536,256]{1,0:T(8,128)}), f32[6144,256]{1,0:T(8,128)}) %all-gather.15.cloned.1.call-update) | async-done | bytes 6291472 | tf_op jit(solution)/shard_map/all_gather | solution.py:133
  488.3 41.7 %gather_fusion.8 = f32[10176,256]{1,0:T(8,128)} fusion(f32[6144,256]{1,0:T(8,128)} %all-gather.15.cloned.1.call-done, s32[10240]{0:T(1024)S(1)} %pad_clamp_fusion), kind=kCustom, calls=%fused_computation.8 | custom fusion | bytes 20881152 | tf_op jit(solution)/shard_map/gather | solution.py:109
  535.6 68.2 %all-gather.17.cloned.1.call-done = f32[6144,256]{1,0:T(8,128)} async-done(((f32[1536,256]{1,0:T(8,128)}), f32[6144,256]{1,0:T(8,128)}) %all-gather.17.cloned.1.call-update) | async-done | bytes 6291472 | tf_op jit(solution)/shard_map/all_gather | solution.py:133
  603.8 41.7 %gather_fusion.10 = f32[10176,256]{1,0:T(8,128)} fusion(f32[6144,256]{1,0:T(8,128)} %all-gather.17.cloned.1.call-done, s32[10240]{0:T(1024)S(1)} %pad_clamp_fusion), kind=kCustom, calls=%fused_computation.10 | custom fusion | bytes 20881152 | tf_op jit(solution)/shard_map/gather | solution.py:109
  744.3 27.7 %gather_fusion.9 = f32[6144,256]{1,0:T(8,128)} fusion(f32[10176,256]{1,0:T(8,128)} %bitcast.32, s32[6144]{0:T(1024)S(1)} %get-tuple-element.27), kind=kCustom, calls=%fused_computation.9 | custom fusion | bytes 12607488 | tf_op jit(solution)/shard_map/gather | solution.py:109
  772.5 27.7 %gather_fusion.11 = f32[6144,256]{1,0:T(8,128)} fusion(f32[10176,256]{1,0:T(8,128)} %bitcast.34, s32[6144]{0:T(1024)S(1)} %get-tuple-element.27), kind=kCustom, calls=%fused_computation.11 | custom fusion | bytes 12607488 | tf_op jit(solution)/shard_map/gather | solution.py:109
  800.2 48.1 %shard_map.68 = (f32[4096,128]{1,0:T(8,128)}, f32[4096,256]{1,0:T(8,128)}, f32[4096,256]{1,0:T(8,128)}, f32[4096,128]{1,0:T(8,128)}, f32[4096,256]{1,0:T(8,128)}...) custom-call(f32[4096,128]{1,0:T(8,128)} %gather_fusion.1, ...), custom_call_target="tpu_custom_call" | custom-call | flops 32212254720 | bytes 52428800 | tf_op jit(solution)/shard_map/pallas_call | solution.py:90
  871.8 45.0 %all_to_all.73 = f32[8,848,128]{2,1,0:T(8,128)} all-to-all(f32[8,848,128]{2,1,0:T(8,128)S(1)} %bitcast.75), channel_id=1, replica_groups={{0,1,2,3,4,5,6,7},{8,9,10,11,12,13,14,15},{16,17,18,19,20,21,22,23},{24..., dimensions={0} | all-to-all | bytes 6946816 | tf_op jit(solution)/shard_map/all_to_all | solution.py:130
  916.8 40.9 %scatter_custom_fusion.1 = f32[6144,128]{1,0:T(8,128)} fusion(s32[6784]{0:T(1024)} %copy-done.5, f32[6784,128]{1,0:T(8,128)} %bitcast.80, f32[]{:T(128)} %constant.139.clone.1), kind=kCustom, calls=%fused_computation.55 | custom fusion | flops 868352 | bytes 3146240 | tf_op jit(solution)/shard_map/scatter-add | solution.py:115
  983.8 84.0 %all_to_all.74 = f32[8,848,256]{2,1,0:T(8,128)} all-to-all(f32[8,848,256]{2,1,0:T(8,128)} %bitcast.73), channel_id=1, replica_groups={{0,1,2,3,4,5,6,7},{8,9,10,11,12,13,14,15},{16,17,18,19,20,21,22,23},{24..., dimensions={0} | all-to-all | bytes 13893632 | tf_op jit(solution)/shard_map/all_to_all | solution.py:130
  1067.9 38.6 %scatter_custom_fusion.3 = f32[6144,256]{1,0:T(8,128)} fusion(s32[6784]{0:T(1024)} %copy-done.5, f32[6784,256]{1,0:T(8,128)} %bitcast.79, f32[]{:T(128)} %constant.139.clone.1), kind=kCustom, calls=%fused_computation.47 | custom fusion | flops 1736704 | bytes 6291968 | tf_op jit(solution)/shard_map/scatter-add | solution.py:115
  1132.9 84.0 %all_to_all.75 = f32[8,848,256]{2,1,0:T(8,128)} all-to-all(f32[8,848,256]{2,1,0:T(8,128)} %bitcast.72), channel_id=1, replica_groups={{0,1,2,3,4,5,6,7},{8,9,10,11,12,13,14,15},{16,17,18,19,20,21,22,23},{24..., dimensions={0} | all-to-all | bytes 13893632 | tf_op jit(solution)/shard_map/all_to_all | solution.py:130
  1216.9 38.6 %scatter_custom_fusion.5 = f32[6144,256]{1,0:T(8,128)} fusion(s32[6784]{0:T(1024)} %copy-done.5, f32[6784,256]{1,0:T(8,128)} %bitcast.78, f32[]{:T(128)} %constant.139.clone.1), kind=kCustom, calls=%fused_computation.45 | custom fusion | flops 1736704 | bytes 6291968 | tf_op jit(solution)/shard_map/scatter-add | solution.py:115
  1301.0 27.3 %scatter_custom_fusion.12 = f32[10176,256]{1,0:T(8,128)} fusion(s32[4096]{0:T(1024)S(1)} %compare_select_fusion.3, f32[4096,256]{1,0:T(8,128)} %get-tuple-element.18, f32[]{:T(128)} %constant.139.clone.1), kind=kCustom, calls=%fused_computation.27 | custom fusion | flops 1048576 | bytes 10420736 | tf_op jit(solution)/shard_map/scatter-add | solution.py:115
  1366.1 57.1 %scatter_custom_fusion.8 = f32[6144,128]{1,0:T(8,128)} fusion(s32[10176]{0:T(1024)} %bitcast.84, f32[10176,128]{1,0:T(8,128)} %bitcast.42, f32[]{:T(128)} %constant.139.clone.1), kind=kCustom, calls=%fused_computation.53 | custom fusion | flops 1302528 | bytes 3146240 | tf_op jit(solution)/shard_map/scatter-add | solution.py:115
  1423.5 58.4 %all-to-all-done.12 = f32[8,1272,256]{2,1,0:T(8,128)} async-done(((f32[8,1272,256]{2,1,0:T(8,128)}), f32[8,1272,256]{2,1,0:T(8,128)}, u32[]{:S(2)}, u32[]{:S(2)}) %all-to-all-start.12) | async-done | bytes 10420256 | tf_op jit(solution)/shard_map/all_to_all | solution.py:130
  1481.9 53.4 %scatter_custom_fusion.14 = f32[6144,256]{1,0:T(8,128)} fusion(s32[10176]{0:T(1024)} %bitcast.85, f32[10176,256]{1,0:T(8,128)} %bitcast.46, f32[]{:T(128)} %constant.139.clone.1), kind=kCustom, calls=%fused_computation.41 | custom fusion | flops 2605056 | bytes 6291968 | tf_op jit(solution)/shard_map/scatter-add | solution.py:115
  1535.3 27.4 %scatter_custom_fusion.9 = f32[10176,256]{1,0:T(8,128)} fusion(s32[4096]{0:T(1024)S(1)} %compare_select_fusion.3, f32[4096,256]{1,0:T(8,128)} %get-tuple-element.16, f32[]{:T(128)} %constant.139.clone.1), kind=kCustom, calls=%fused_computation.29 | custom fusion | flops 1048576 | bytes 10420736 | tf_op jit(solution)/shard_map/scatter-add | solution.py:115
  1582.2 122.1 %all_to_all.76 = f32[8,1272,256]{2,1,0:T(8,128)} all-to-all(f32[8,1272,256]{2,1,0:T(8,128)} %bitcast.64), channel_id=1, replica_groups={{0,1,2,3,4,5,6,7},{8,9,10,11,12,13,14,15},{16,17,18,19,20,21,22,23},{24..., dimensions={0} | all-to-all | bytes 20840448 | tf_op jit(solution)/shard_map/all_to_all | solution.py:130
  1704.3 53.4 %scatter_custom_fusion.11 = f32[6144,256]{1,0:T(8,128)} fusion(s32[10176]{0:T(1024)} %bitcast.86, f32[10176,256]{1,0:T(8,128)} %bitcast.77, f32[]{:T(128)} %constant.139.clone.1), kind=kCustom, calls=%fused_computation.43 | custom fusion | flops 2605056 | bytes 6291968 | tf_op jit(solution)/shard_map/scatter-add | solution.py:115
  1768.9 98.4 %reduce-scatter.15.cloned.1.call-done = f32[1536,256]{1,0:T(8,128)} async-done(((f32[6144,256]{1,0:T(8,128)}), f32[1536,256]{1,0:T(8,128)}) %reduce-scatter.15.cloned.1.call-update) | async-done | bytes 1572880 | tf_op jit(solution)/shard_map/reduce_scatter | solution.py:136
  (169 shorter events, 450.2 us)
Async XLA Ops:
  7.2 103.3 %all-gather.7.cloned.1.call-start = ((), (), s32[]{:S(2)}) async-start(), calls=%async_computation.19 | async-start | bytes 3932160 | tf_op jit(solution)/shard_map/all_gather | solution.py:133
  14.6 127.4 %all-gather.13.cloned.1.call-start = ((), (), s32[]{:S(2)}) async-start(), calls=%async_computation.22 | async-start | bytes 3932160 | tf_op jit(solution)/shard_map/all_gather | solution.py:133
  20.1 28.3 %copy-start.10 = (s32[4096]{0:T(1024)S(1)}, s32[4096]{0:T(1024)}, u32[]{:S(2)}) copy-start(s32[4096]{0:T(1024)} %param.8) | copy-start | bytes 49156
  20.1 28.3 %copy-start.11 = (s32[2048]{0:T(1024)S(1)}, s32[2048]{0:T(1024)}, u32[]{:S(2)}) copy-start(s32[2048]{0:T(1024)} %param.9) | copy-start | bytes 24580
  22.3 235.0 %all-gather.11.cloned.1.call-start = ((), (), s32[]{:S(2)}) async-start(), calls=%async_computation.21 | async-start | bytes 7864320 | tf_op jit(solution)/shard_map/all_gather | solution.py:133
  125.9 52.3 %all-to-all-start.1 = ((f32[8,848,128]{2,1,0:T(8,128)}), f32[8,848,128]{2,1,0:T(8,128)S(1)}, u32[]{:S(2)}, u32[]{:S(2)}) async-start(f32[8,848,128]{2,1,0:T(8,128)} %bitcast.76), calls=%async_computation.1 | async-start | bytes 6946816 | tf_op jit(solution)/shard_map/all_to_all | solution.py:130
  129.6 243.2 %all-gather.9.cloned.1.call-start = ((), (), s32[]{:S(2)}) async-start(), calls=%async_computation.20 | async-start | bytes 7864320 | tf_op jit(solution)/shard_map/all_gather | solution.py:133
  178.2 98.9 %all-to-all-start.4 = ((f32[8,1272,128]{2,1,0:T(8,128)}), f32[8,1272,128]{2,1,0:T(8,128)}, u32[]{:S(2)}, u32[]{:S(2)}) async-start(f32[8,1272,128]{2,1,0:T(8,128)} %bitcast.74), calls=%async_computation.4 | async-start | bytes 10420224 | tf_op jit(solution)/shard_map/all_to_all | solution.py:130
  277.1 115.6 %all-to-all-start.3 = ((f32[8,848,256]{2,1,0:T(8,128)}), f32[8,848,256]{2,1,0:T(8,128)}, u32[]{:S(2)}, u32[]{:S(2)}) async-start(f32[8,848,256]{2,1,0:T(8,128)} %bitcast.71), calls=%async_computation.3 | async-start | bytes 13893632 | tf_op jit(solution)/shard_map/all_to_all | solution.py:130
  281.9 206.3 %all-gather.15.cloned.1.call-start = ((), (), s32[]{:S(2)}) async-start(), calls=%async_computation.23 | async-start | bytes 7864320 | tf_op jit(solution)/shard_map/all_gather | solution.py:133
  392.7 137.3 %all-to-all-start.2 = ((f32[8,848,256]{2,1,0:T(8,128)}), f32[8,848,256]{2,1,0:T(8,128)}, u32[]{:S(2)}, u32[]{:S(2)}) async-start(f32[8,848,256]{2,1,0:T(8,128)} %bitcast.70), calls=%async_computation.2 | async-start | bytes 13893632 | tf_op jit(solution)/shard_map/all_to_all | solution.py:130
  397.5 206.3 %all-gather.17.cloned.1.call-start = ((), (), s32[]{:S(2)}) async-start(), calls=%async_computation.24 | async-start | bytes 7864320 | tf_op jit(solution)/shard_map/all_gather | solution.py:133
  530.0 121.4 %all-to-all-start.5 = ((f32[8,1272,256]{2,1,0:T(8,128)}), f32[8,1272,256]{2,1,0:T(8,128)}, u32[]{:S(2)}, u32[]{:S(2)}) async-start(f32[8,1272,256]{2,1,0:T(8,128)} %bitcast.69), calls=%async_computation.5 | async-start | bytes 20840448 | tf_op jit(solution)/shard_map/all_to_all | solution.py:130
  651.5 121.1 %all-to-all-start.6 = ((f32[8,1272,256]{2,1,0:T(8,128)}), f32[8,1272,256]{2,1,0:T(8,128)}, u32[]{:S(2)}, u32[]{:S(2)}) async-start(f32[8,1272,256]{2,1,0:T(8,128)} %bitcast.68), calls=%async_computation.6 | async-start | bytes 20840448 | tf_op jit(solution)/shard_map/all_to_all | solution.py:130
  656.7 1101.0 %reduce-scatter.7.cloned.1.call-start = ((), (), s32[]{:S(2)}) async-start(), calls=%async_computation.25 | async-start | bytes 3932160 | tf_op jit(solution)/shard_map/reduce_scatter | solution.py:136
  957.7 800.0 %reduce-scatter.9.cloned.1.call-start = ((), (), s32[]{:S(2)}) async-start(), calls=%async_computation.26 | async-start | bytes 7864320 | tf_op jit(solution)/shard_map/reduce_scatter | solution.py:136
  1106.5 651.2 %reduce-scatter.11.cloned.1.call-start = ((), (), s32[]{:S(2)}) async-start(), calls=%async_computation.27 | async-start | bytes 7864320 | tf_op jit(solution)/shard_map/reduce_scatter | solution.py:136
  1216.9 38.6 %copy-start.6 = (s32[6144]{0:T(1024)S(1)}, s32[6144]{0:T(1024)}, u32[]{:S(2)}) copy-start(s32[6144]{0:T(1024)} %get-tuple-element.26) | copy-start | bytes 73732
  1295.9 65.1 %all-to-all-start.10 = ((f32[8,1272,128]{2,1,0:T(8,128)}), f32[8,1272,128]{2,1,0:T(8,128)}, u32[]{:S(2)}, u32[]{:S(2)}) async-start(f32[8,1272,128]{2,1,0:T(8,128)} %bitcast.67), calls=%async_computation.13 | async-start | bytes 10420224 | tf_op jit(solution)/shard_map/all_to_all | solution.py:130
  1360.9 121.0 %all-to-all-start.12 = ((f32[8,1272,256]{2,1,0:T(8,128)}), f32[8,1272,256]{2,1,0:T(8,128)}, u32[]{:S(2)}, u32[]{:S(2)}) async-start(f32[8,1272,256]{2,1,0:T(8,128)} %bitcast.65), calls=%async_computation.17 | async-start | bytes 20840448 | tf_op jit(solution)/shard_map/all_to_all | solution.py:130
  1366.1 402.8 %reduce-scatter.13.cloned.1.call-start = ((), (), s32[]{:S(2)}) async-start(), calls=%async_computation.28 | async-start | bytes 3932160 | tf_op jit(solution)/shard_map/reduce_scatter | solution.py:136
  1423.3 345.6 %reduce-scatter.17.cloned.1.call-start = ((), (), s32[]{:S(2)}) async-start(), calls=%async_computation.30 | async-start | bytes 7864320 | tf_op jit(solution)/shard_map/reduce_scatter | solution.py:136
  1535.3 332.0 %reduce-scatter.15.cloned.1.call-start = ((), (), s32[]{:S(2)}) async-start(), calls=%async_computation.29 | async-start | bytes 7864320 | tf_op jit(solution)/shard_map/reduce_scatter | solution.py:136
  1535.3 27.4 %copy-start = (f32[2048,256]{1,0:T(8,128)S(1)}, f32[2048,256]{1,0:T(8,128)}, u32[]{:S(2)}) copy-start(f32[2048,256]{1,0:T(8,128)} %get-tuple-element.17) | copy-start | bytes 6291460
  (9 other events, 81.3 us)
Sparse Core Ops, SparseCore 0:
  14.7 61.8 all-gather.6
  78.2 63.8 all-gather.12
  143.6 113.5 all-gather.10
  259.2 113.5 all-gather.8
  374.8 113.4 all-gather.14
  490.3 113.4 all-gather.16
  957.8 58.4 reduce-scatter.6
  1106.6 109.4 reduce-scatter.8
  1255.6 109.5 reduce-scatter.10
  1423.4 60.6 reduce-scatter.12
  1535.4 109.4 reduce-scatter.16
  1757.8 109.4 reduce-scatter.14

commit v3 on v2

--- a/solution.py
+++ b/solution.py
@@ -18,6 +18,7 @@
 LANES = 128
 CUTS = (0, 128, 384)
 CHUNKS = range(len(CUTS))
+BACK_CUTS = {'in': (0, 256), 'out': (0, 128, 384)}
 PAIR_BLOCK = 512
 
 
@@ -52,52 +53,71 @@
     return cell_of_id, jnp.stack(asks)
 
 
-def pair_kernel(neg_scale, bounds, *refs):
-    n = len(bounds)
-    center, context, negative, d_center, d_context, d_negative = (refs[k * n:(k + 1) * n] for k in range(6))
-    neg_half = refs[6 * n]
+def pair_kernel(neg_scale, counts, *refs):
+    groups, at = [], 0
+    for n in counts:
+        groups.append(refs[at:at + n])
+        at += n
+    center, context, negative, d_center, d_out = groups
+    neg_half, d_negative = refs[at:]
+    step = pl.program_id(0)
+    block = center[0].shape[0]
+    blocks = pl.num_programs(0) - d_negative.shape[0] // block
 
-    @pl.when(pl.program_id(0) == 0)
+    def put(chunks, values):
+        lo = 0
+        for c in chunks:
+            c[...] = values[:, lo:lo + c.shape[1]]
+            lo += c.shape[1]
+
+    @pl.when(step == 0)
     def _():
-        for k, (lo, hi) in enumerate(bounds):
-            neg_half[:, lo:hi] = negative[k][...].astype(jnp.bfloat16)
-            d_negative[k][...] = jnp.zeros_like(d_negative[k])
+        neg_half[...] = jnp.concatenate([r[...].astype(jnp.bfloat16) for r in negative], axis=1)
+        d_negative[...] = jnp.zeros_like(d_negative)
 
-    u = [r[...] for r in center]
-    v = [r[...] for r in context]
-    pos_score = sum(jnp.sum(a * b, axis=1, keepdims=True) for a, b in zip(u, v))
-    pos_grad = jax.nn.sigmoid(pos_score) - 1.0
-    center_half = jnp.concatenate([a.astype(jnp.bfloat16) for a in u], axis=1)
-    neg_score = lax.dot_general(center_half, neg_half[...], (((1,), (1,)), ((), ())), preferred_element_type=jnp.float32)
-    neg_grad = (neg_scale * jax.nn.sigmoid(neg_score)).astype(jnp.bfloat16)
-    from_neg = jnp.dot(neg_grad, neg_half[...], preferred_element_type=jnp.float32)
-    to_neg = lax.dot_general(neg_grad, center_half, (((0,), (0,)), ((), ())), preferred_element_type=jnp.float32)
-    for k, (lo, hi) in enumerate(bounds):
-        d_context[k][...] = pos_grad * u[k]
-        d_center[k][...] = pos_grad * v[k] + from_neg[:, lo:hi]
-        d_negative[k][...] += to_neg[:, lo:hi]
+    @pl.when(step < blocks)
+    def _():
+        u = jnp.concatenate([r[...] for r in center], axis=1)
+        v = jnp.concatenate([r[...] for r in context], axis=1)
+        pos_grad = jax.nn.sigmoid(jnp.sum(u * v, axis=1, keepdims=True)) - 1.0
+        center_half = u.astype(jnp.bfloat16)
+        neg_score = lax.dot_general(center_half, neg_half[...], (((1,), (1,)), ((), ())), preferred_element_type=jnp.float32)
+        neg_grad = (neg_scale * jax.nn.sigmoid(neg_score)).astype(jnp.bfloat16)
+        put(d_center, pos_grad * v + jnp.dot(neg_grad, neg_half[...], preferred_element_type=jnp.float32))
+        put(d_out, pos_grad * u)
+        d_negative[...] += lax.dot_general(neg_grad, center_half, (((0,), (0,)), ((), ())), preferred_element_type=jnp.float32)
+
+    @pl.when(step >= blocks)
+    def _():
+        put(d_out, d_negative[pl.ds(pl.multiple_of((step - blocks) * block, block), block), :])
 
 
 def pair_grads(center, looked_up):
-    pairs, negs = center[0].shape[0], looked_up[0].shape[0] - center[0].shape[0]
+    pairs, rows = center[0].shape[0], looked_up[0].shape[0]
+    negs = rows - pairs
     widths = [c.shape[1] for c in center]
-    total, n = sum(widths), len(widths)
-    bounds = [(sum(widths[:k]), sum(widths[:k + 1])) for k in range(n)]
-    pair_specs = [pl.BlockSpec((PAIR_BLOCK, w), lambda i: (i, 0)) for w in widths]
-    neg_in_specs = [pl.BlockSpec((negs, w), lambda i: (pairs // negs, 0)) for w in widths]
-    neg_out_specs = [pl.BlockSpec((negs, w), lambda i: (0, 0)) for w in widths]
-    shapes = [jax.ShapeDtypeStruct((m, w), jnp.float32) for m in (pairs, pairs, negs) for w in widths]
+    total = sum(widths)
+    back = {side: chunk_widths(BACK_CUTS[side], total) for side in ('in', 'out')}
+    last = pairs // PAIR_BLOCK - 1
+    specs = [pl.BlockSpec((PAIR_BLOCK, w), lambda i: (jnp.minimum(i, last), 0)) for w in widths]
+    neg_specs = [pl.BlockSpec((negs, w), lambda i: (pairs // negs, 0)) for w in widths]
+    in_specs = [pl.BlockSpec((PAIR_BLOCK, w), lambda i: (jnp.minimum(i, last), 0)) for w in back['in']]
+    out_specs = [pl.BlockSpec((PAIR_BLOCK, w), lambda i: (i, 0)) for w in back['out']]
     grads = pl.pallas_call(
-        functools.partial(pair_kernel, NEG_WEIGHT / negs, bounds),
-        grid=(pairs // PAIR_BLOCK,),
-        in_specs=pair_specs + pair_specs + neg_in_specs,
-        out_specs=pair_specs + pair_specs + neg_out_specs,
-        out_shape=shapes,
-        scratch_shapes=[pltpu.VMEM((negs, total), jnp.bfloat16)],
+        functools.partial(pair_kernel, NEG_WEIGHT / negs, [len(widths)] * 3 + [len(back['in']), len(back['out'])]),
+        grid=(rows // PAIR_BLOCK,),
+        in_specs=specs + specs + neg_specs,
+        out_specs=in_specs + out_specs,
+        out_shape=[jax.ShapeDtypeStruct((m, w), jnp.float32) for side, m in (('in', pairs), ('out', rows)) for w in back[side]],
+        scratch_shapes=[pltpu.VMEM((negs, total), jnp.bfloat16), pltpu.VMEM((negs, total), jnp.float32)],
         compiler_params=pltpu.CompilerParams(dimension_semantics=('arbitrary',), vmem_limit_bytes=60 * 2 ** 20),
         cost_estimate=pl.CostEstimate(flops=6 * pairs * negs * total, bytes_accessed=4 * total * (4 * pairs + 2 * negs), transcendentals=2 * pairs * negs),
     )(*center, *looked_up, *looked_up)
-    return grads[:n], grads[n:2 * n], grads[2 * n:]
+    return {'in': grads[:len(back['in'])], 'out': grads[len(back['in']):]}
+
+
+def chunk_widths(cuts, total):
+    return [hi - lo for lo, hi in zip(cuts, cuts[1:] + (total,))]
 
 
 def column_chunks(shard):
@@ -109,15 +129,12 @@
     return table.at[rows].get(mode='promise_in_bounds')
 
 
-def add_rows(num_rows, *parts):
-    total = jnp.zeros((num_rows, parts[0][1].shape[1]), parts[0][1].dtype)
-    for rows, values in parts:
-        total = total.at[rows].add(values, mode='promise_in_bounds')
-    return total
+def add_rows(num_rows, rows, values):
+    return jnp.zeros((num_rows, values.shape[1]), values.dtype).at[rows].add(values, mode='promise_in_bounds')
 
 
 FETCH_ORDER = [('out', k) for k in CHUNKS] + [('in', k) for k in reversed(CHUNKS)]
-BACK_ORDER = FETCH_ORDER[::-1]
+BACK_ORDER = [('in', k) for k in range(len(BACK_CUTS['in']))] + [('out', k) for k in reversed(range(len(BACK_CUTS['out'])))]
 
 
 def solution(mesh):
@@ -156,17 +173,16 @@
             found = take_rows(column[side, k], asked[side]).reshape(PLANE, capacity[side], -1)
             returned = exchange(found)
             looked_up[side, k] = take_rows(returned.reshape(-1, returned.shape[2]), cell[side])
-        d_center, d_context, d_negative = pair_grads([looked_up['in', k] for k in CHUNKS], [looked_up['out', k] for k in CHUNKS])
+        grads = pair_grads([looked_up['in', k] for k in CHUNKS], [looked_up['out', k] for k in CHUNKS])
         row_sum = {}
         for side, k in BACK_ORDER:
-            parts = [(in_cell, d_center[k])] if side == 'in' else [(out_cell[:pairs_dev], d_context[k]), (out_cell[pairs_dev:], d_negative[k])]
-            cells = add_rows(PLANE * capacity[side], *parts)
+            cells = add_rows(PLANE * capacity[side], cell[side], grads[side][k])
             arrived = exchange(cells.reshape(PLANE, capacity[side], -1))
-            dense = add_rows(num_rows, (asked[side], arrived.reshape(-1, arrived.shape[2])))
+            dense = add_rows(num_rows, asked[side], arrived.reshape(-1, arrived.shape[2]))
             row_sum[side, k] = sum_lines(dense)
         new = []
         for side, old in (('in', in_shard), ('out', out_shard)):
-            grad = jnp.concatenate([row_sum[side, k] for k in CHUNKS], axis=1)[:, :dim]
+            grad = jnp.concatenate([row_sum[side, k] for k in range(len(BACK_CUTS[side]))], axis=1)[:, :dim]
             new.append(old - LEARN_RATE * grad)
         return tuple(new)
 

time: 1900 us -> 1880 us (0.989)
  other arithmetic: 540 us -> 466 us
  waiting for transfers between devices: 502 us -> 560 us
    scatter-add x15 -> x10, other arithmetic: 491 us -> 418 us  [add_rows(): jnp.zeros((num_rows, values.shape[1]), values.dtype).at[rows]]
    reduce_scatter x6 -> x5, waiting for transfers between devices: 98.4 us -> 149 us  [sum_lines(): lax.psum_scatter(column, AXIS_NAME, scatter_dimension=0, axis_index_group...]
    all_to_all x5 -> x4, blocking collectives: 344 us -> 337 us  [exchange(): lax.all_to_all(cells, AXIS_NAME, 0, 0, axis_index_groups=plane_groups)]
  transfers between devices with their start and end apart: 20 -> 19, of which waited for: 10 -> 10; matrix products, arithmetic and copies ran while one was open for 41% -> 39% of each run, Pallas kernels for 0% -> 0%
where the time goes in v3:
time: 1880 us; the launch traced here: 1860 us
  waiting for transfers between devices  560 us (30%)
  other arithmetic  466 us (25%)
  local copies, waits for them, and re-layouts  347 us (18%)
  blocking collectives  337 us (18%)
  between operations  65.2 us (3%)
  Pallas kernels  49.9 us (3%)
  starting transfers between devices  39.5 us (2%)
    scatter-add x10, other arithmetic, add_rows(): jnp.zeros((num_rows, values.shape[1]), values.dtype).at[rows]  418 us
    all_to_all x4, blocking collectives, exchange(): lax.all_to_all(cells, AXIS_NAME, 0, 0, axis_index_groups=plane_groups)  337 us
    all_gather x6, waiting for transfers between devices, gather_lines(): lax.all_gather(shard, AXIS_NAME, axis_index_groups=line_groups, tiled=True)  324 us
    gather x12, local copies, waits for them, and re-layouts, take_rows(): return table.at[rows].get(mode='promise_in_bounds')  306 us
    reduce_scatter x5, waiting for transfers between devices, sum_lines(): lax.psum_scatter(column, AXIS_NAME, scatter_dimension=0, axis_index_group...  149 us
    all_to_all x8, waiting for transfers between devices, exchange(): lax.all_to_all(cells, AXIS_NAME, 0, 0, axis_index_groups=plane_groups)  86.6 us
    pallas_call x1, Pallas kernels, pair_grads(): pl.pallas_call(functools.partial(pair_kernel, NEG_WEIGHT / negs, [len(wid...  49.9 us
    all_to_all x8, starting transfers between devices, exchange(): lax.all_to_all(cells, AXIS_NAME, 0, 0, axis_index_groups=plane_groups)  38.9 us
  transfers between devices with their start and end apart: 19, of which 10 were waited for; matrix products, arithmetic and copies ran while one was open for 39% of the time, Pallas kernels for 0%

profile of v3, /device:TPU:24, one launch (start us, length us, event | category | flops | bytes accessed | tf_op | source)
XLA Modules:
  0.0 1864.7 jit_solution(3115332202167234182)
XLA Ops:
  141.4 36.1 %gather_fusion.6 = f32[10176,128]{1,0:T(8,128)} fusion(f32[6144,128]{1,0:T(8,128)} %all-gather.13.cloned.1.call-done, s32[10240]{0:T(1024)S(1)} %pad_clamp_fusion), kind=kCustom, calls=%fused_computation.6 | custom fusion | bytes 10460928 | tf_op jit(solution)/shard_map/gather | solution.py:129
  182.2 74.3 %all-gather.11.cloned.1.call-done = f32[6144,256]{1,0:T(8,128)} async-done(((f32[1536,256]{1,0:T(8,128)}), f32[6144,256]{1,0:T(8,128)}) %all-gather.11.cloned.1.call-update) | async-done | bytes 6291472 | tf_op jit(solution)/shard_map/all_gather | solution.py:150
  284.1 88.0 %all-gather.9.cloned.1.call-done = f32[6144,256]{1,0:T(8,128)} async-done(((f32[1536,256]{1,0:T(8,128)}), f32[6144,256]{1,0:T(8,128)}) %all-gather.9.cloned.1.call-update) | async-done | bytes 6291472 | tf_op jit(solution)/shard_map/all_gather | solution.py:150
  399.6 88.0 %all-gather.15.cloned.1.call-done = f32[6144,256]{1,0:T(8,128)} async-done(((f32[1536,256]{1,0:T(8,128)}), f32[6144,256]{1,0:T(8,128)}) %all-gather.15.cloned.1.call-update) | async-done | bytes 6291472 | tf_op jit(solution)/shard_map/all_gather | solution.py:150
  487.6 41.7 %gather_fusion.8 = f32[10176,256]{1,0:T(8,128)} fusion(f32[6144,256]{1,0:T(8,128)} %all-gather.15.cloned.1.call-done, s32[10240]{0:T(1024)S(1)} %pad_clamp_fusion), kind=kCustom, calls=%fused_computation.8 | custom fusion | bytes 20881152 | tf_op jit(solution)/shard_map/gather | solution.py:129
  534.6 68.5 %all-gather.17.cloned.1.call-done = f32[6144,256]{1,0:T(8,128)} async-done(((f32[1536,256]{1,0:T(8,128)}), f32[6144,256]{1,0:T(8,128)}) %all-gather.17.cloned.1.call-update) | async-done | bytes 6291472 | tf_op jit(solution)/shard_map/all_gather | solution.py:150
  603.1 41.7 %gather_fusion.10 = f32[10176,256]{1,0:T(8,128)} fusion(f32[6144,256]{1,0:T(8,128)} %all-gather.17.cloned.1.call-done, s32[10240]{0:T(1024)S(1)} %pad_clamp_fusion), kind=kCustom, calls=%fused_computation.10 | custom fusion | bytes 20881152 | tf_op jit(solution)/shard_map/gather | solution.py:129
  743.2 27.7 %gather_fusion.9 = f32[6144,256]{1,0:T(8,128)} fusion(f32[10176,256]{1,0:T(8,128)} %bitcast.32, s32[6144]{0:T(1024)S(1)} %get-tuple-element.19), kind=kCustom, calls=%fused_computation.9 | custom fusion | bytes 12607488 | tf_op jit(solution)/shard_map/gather | solution.py:129
  771.5 27.7 %gather_fusion.11 = f32[6144,256]{1,0:T(8,128)} fusion(f32[10176,256]{1,0:T(8,128)} %bitcast.34, s32[6144]{0:T(1024)S(1)} %get-tuple-element.19), kind=kCustom, calls=%fused_computation.11 | custom fusion | bytes 12607488 | tf_op jit(solution)/shard_map/gather | solution.py:129
  799.2 49.9 %shard_map.68 = (f32[4096,256]{1,0:T(8,128)}, f32[4096,384]{1,0:T(8,128)}, f32[6144,128]{1,0:T(8,128)}, f32[6144,256]{1,0:T(8,128)}, f32[6144,256]{1,0:T(8,128)}) custom-call(f32[4096,128]{1,0:T(8,128)} %gather_fusion.1, f32[4096,256]{1,0:T(8,128)} %gather_fusion.3, f32[4096,256]{1,0:T(8,128)} %gather_fusion.5, f32[6144,128]{1,0:T(8,128)} %gather_fusion.7, ...), custom_call_target="tpu_custom_call" | custom-call | flops 32212254720 | bytes 52428800 | tf_op jit(solution)/shard_map/pallas_call | solution.py:106
  849.1 36.1 %scatter_custom_fusion.4 = f32[10176,128]{1,0:T(8,128)} fusion(s32[6144]{0:T(1024)} %get-tuple-element.18, f32[6144,128]{1,0:T(8,128)} %get-tuple-element.9, f32[]{:T(128)} %constant.137.clone.1), kind=kCustom, calls=%fused_computation.43 | custom fusion | flops 786432 | bytes 5210624 | tf_op jit(solution)/shard_map/scatter-add | solution.py:133
  890.3 38.2 %scatter_custom_fusion.8 = f32[10176,256]{1,0:T(8,128)} fusion(s32[6144]{0:T(1024)} %get-tuple-element.18, f32[6144,256]{1,0:T(8,128)} %get-tuple-element.11, f32[]{:T(128)} %constant.137.clone.1), kind=kCustom, calls=%fused_computation.22 | custom fusion | flops 1572864 | bytes 10420736 | tf_op jit(solution)/shard_map/scatter-add | solution.py:133
  955.5 57.1 %scatter_custom_fusion.5 = f32[6144,128]{1,0:T(8,128)} fusion(s32[10176]{0:T(1024)} %bitcast.80, f32[10176,128]{1,0:T(8,128)} %bitcast.40, f32[]{:T(128)} %constant.137.clone.1), kind=kCustom, calls=%fused_computation.45 | custom fusion | flops 1302528 | bytes 3146240 | tf_op jit(solution)/shard_map/scatter-add | solution.py:133
  1012.7 58.6 %all-to-all-done.11 = f32[8,1272,256]{2,1,0:T(8,128)} async-done(((f32[8,1272,256]{2,1,0:T(8,128)}), f32[8,1272,256]{2,1,0:T(8,128)}, u32[]{:S(2)}, u32[]{:S(2)}) %all-to-all-start.11) | async-done | bytes 10420256 | tf_op jit(solution)/shard_map/all_to_all | solution.py:147
  1071.3 53.4 %scatter_custom_fusion.9 = f32[6144,256]{1,0:T(8,128)} fusion(s32[10176]{0:T(1024)} %bitcast.81, f32[10176,256]{1,0:T(8,128)} %bitcast.44, f32[]{:T(128)} %constant.137.clone.1), kind=kCustom, calls=%fused_computation.37 | custom fusion | flops 2605056 | bytes 6291968 | tf_op jit(solution)/shard_map/scatter-add | solution.py:133
  1124.9 38.3 %scatter_custom_fusion.6 = f32[10176,256]{1,0:T(8,128)} fusion(s32[6144]{0:T(1024)} %get-tuple-element.18, f32[6144,256]{1,0:T(8,128)} %get-tuple-element.10, f32[]{:T(128)} %constant.137.clone.1), kind=kCustom, calls=%fused_computation.24 | custom fusion | flops 1572864 | bytes 10420736 | tf_op jit(solution)/shard_map/scatter-add | solution.py:133
  1163.2 121.9 %all_to_all.68 = f32[8,1272,256]{2,1,0:T(8,128)} all-to-all(f32[8,1272,256]{2,1,0:T(8,128)} %bitcast.66), channel_id=1, replica_groups={{0,1,2,3,4,5,6,7},{8,9,10,11,12,13,14,15},{16,17,18,19,20,21,22,23},{24..., dimensions={0} | all-to-all | bytes 20840448 | tf_op jit(solution)/shard_map/all_to_all | solution.py:147
  1285.0 53.4 %scatter_custom_fusion.7 = f32[6144,256]{1,0:T(8,128)} fusion(s32[10176]{0:T(1024)} %bitcast.82, f32[10176,256]{1,0:T(8,128)} %bitcast.75, f32[]{:T(128)} %constant.137.clone.1), kind=kCustom, calls=%fused_computation.39 | custom fusion | flops 2605056 | bytes 6291968 | tf_op jit(solution)/shard_map/scatter-add | solution.py:133
  1364.5 84.3 %all_to_all.69 = f32[8,848,256]{2,1,0:T(8,128)} all-to-all(f32[8,848,256]{2,1,0:T(8,128)} %bitcast.70), channel_id=1, replica_groups={{0,1,2,3,4,5,6,7},{8,9,10,11,12,13,14,15},{16,17,18,19,20,21,22,23},{24..., dimensions={0} | all-to-all | bytes 13893632 | tf_op jit(solution)/shard_map/all_to_all | solution.py:147
  1448.8 38.6 %scatter_custom_fusion.1 = f32[6144,256]{1,0:T(8,128)} fusion(s32[6784]{0:T(1024)} %copy-done.2, f32[6784,256]{1,0:T(8,128)} %bitcast.76, f32[]{:T(128)} %constant.137.clone.1), kind=kCustom, calls=%fused_computation.41 | custom fusion | flops 1736704 | bytes 6291968 | tf_op jit(solution)/shard_map/scatter-add | solution.py:133
  1487.4 29.7 %scatter_custom_fusion.2 = f32[6784,384]{1,0:T(8,128)} fusion(s32[4096]{0:T(1024)} %get-tuple-element.33, f32[4096,384]{1,0:T(8,128)} %get-tuple-element.8, f32[]{:T(128)} %constant.137.clone.1), kind=kCustom, calls=%fused_computation.26 | custom fusion | flops 1572864 | bytes 10420736 | tf_op jit(solution)/shard_map/scatter-add | solution.py:133
  1517.1 122.2 %all_to_all.70 = f32[8,848,384]{2,1,0:T(8,128)} all-to-all(f32[8,848,384]{2,1,0:T(8,128)} %bitcast.67), channel_id=1, replica_groups={{0,1,2,3,4,5,6,7},{8,9,10,11,12,13,14,15},{16,17,18,19,20,21,22,23},{24..., dimensions={0} | all-to-all | bytes 20840448 | tf_op jit(solution)/shard_map/all_to_all | solution.py:147
  1639.3 47.2 %scatter_custom_fusion.3 = f32[6144,384]{1,0:T(8,128)} fusion(s32[6784]{0:T(1024)} %copy-done.2, f32[6784,384]{1,0:T(8,128)} %bitcast.74, f32[]{:T(128)} %constant.137.clone.1), kind=kCustom, calls=%fused_computation.28 | custom fusion | flops 2605056 | bytes 9437696 | tf_op jit(solution)/shard_map/scatter-add | solution.py:133
  1697.7 149.2 %reduce-scatter.8.cloned.1.call-done = f32[1536,384]{1,0:T(8,128)} async-done(((f32[6144,384]{1,0:T(8,128)}), f32[1536,384]{1,0:T(8,128)}) %reduce-scatter.8.cloned.1.call-update) | async-done | bytes 2359312 | tf_op jit(solution)/shard_map/reduce_scatter | solution.py:153
  (150 shorter events, 328.0 us)
Async XLA Ops:
  7.2 103.8 %all-gather.7.cloned.1.call-start = ((), (), s32[]{:S(2)}) async-start(), calls=%async_computation.17 | async-start | bytes 3932160 | tf_op jit(solution)/shard_map/all_gather | solution.py:150
  14.6 7.7 slice-start
  14.6 126.7 %all-gather.13.cloned.1.call-start = ((), (), s32[]{:S(2)}) async-start(), calls=%async_computation.20 | async-start | bytes 3932160 | tf_op jit(solution)/shard_map/all_gather | solution.py:150
  20.1 28.1 %copy-start.6 = (s32[4096]{0:T(1024)S(1)}, s32[4096]{0:T(1024)}, u32[]{:S(2)}) copy-start(s32[4096]{0:T(1024)} %param.8) | copy-start | bytes 49156
  20.1 28.1 %copy-start.7 = (s32[2048]{0:T(1024)S(1)}, s32[2048]{0:T(1024)}, u32[]{:S(2)}) copy-start(s32[2048]{0:T(1024)} %param.9) | copy-start | bytes 24580
  22.2 234.3 %all-gather.11.cloned.1.call-start = ((), (), s32[]{:S(2)}) async-start(), calls=%async_computation.19 | async-start | bytes 7864320 | tf_op jit(solution)/shard_map/all_gather | solution.py:150
  126.4 51.1 %all-to-all-start.1 = ((f32[8,848,128]{2,1,0:T(8,128)}), f32[8,848,128]{2,1,0:T(8,128)S(1)}, u32[]{:S(2)}, u32[]{:S(2)}) async-start(f32[8,848,128]{2,1,0:T(8,128)} %bitcast.73), calls=%async_computation.1 | async-start | bytes 6946816 | tf_op jit(solution)/shard_map/all_to_all | solution.py:147
  130.1 241.9 %all-gather.9.cloned.1.call-start = ((), (), s32[]{:S(2)}) async-start(), calls=%async_computation.18 | async-start | bytes 7864320 | tf_op jit(solution)/shard_map/all_gather | solution.py:150
  177.5 98.9 %all-to-all-start.4 = ((f32[8,1272,128]{2,1,0:T(8,128)}), f32[8,1272,128]{2,1,0:T(8,128)}, u32[]{:S(2)}, u32[]{:S(2)}) async-start(f32[8,1272,128]{2,1,0:T(8,128)} %bitcast.71), calls=%async_computation.4 | async-start | bytes 10420224 | tf_op jit(solution)/shard_map/all_to_all | solution.py:147
  276.4 115.5 %all-to-all-start.3 = ((f32[8,848,256]{2,1,0:T(8,128)}), f32[8,848,256]{2,1,0:T(8,128)}, u32[]{:S(2)}, u32[]{:S(2)}) async-start(f32[8,848,256]{2,1,0:T(8,128)} %bitcast.69), calls=%async_computation.3 | async-start | bytes 13893632 | tf_op jit(solution)/shard_map/all_to_all | solution.py:147
  281.3 206.3 %all-gather.15.cloned.1.call-start = ((), (), s32[]{:S(2)}) async-start(), calls=%async_computation.21 | async-start | bytes 7864320 | tf_op jit(solution)/shard_map/all_gather | solution.py:150
  391.9 137.3 %all-to-all-start.2 = ((f32[8,848,256]{2,1,0:T(8,128)}), f32[8,848,256]{2,1,0:T(8,128)}, u32[]{:S(2)}, u32[]{:S(2)}) async-start(f32[8,848,256]{2,1,0:T(8,128)} %bitcast.68), calls=%async_computation.2 | async-start | bytes 13893632 | tf_op jit(solution)/shard_map/all_to_all | solution.py:147
  396.7 206.4 %all-gather.17.cloned.1.call-start = ((), (), s32[]{:S(2)}) async-start(), calls=%async_computation.22 | async-start | bytes 7864320 | tf_op jit(solution)/shard_map/all_gather | solution.py:150
  529.2 121.2 %all-to-all-start.5 = ((f32[8,1272,256]{2,1,0:T(8,128)}), f32[8,1272,256]{2,1,0:T(8,128)}, u32[]{:S(2)}, u32[]{:S(2)}) async-start(f32[8,1272,256]{2,1,0:T(8,128)} %bitcast.64), calls=%async_computation.5 | async-start | bytes 20840448 | tf_op jit(solution)/shard_map/all_to_all | solution.py:147
  650.4 5.3 copy-start.4
  650.4 10.2 copy-start.3
  650.4 121.1 %all-to-all-start.6 = ((f32[8,1272,256]{2,1,0:T(8,128)}), f32[8,1272,256]{2,1,0:T(8,128)}, u32[]{:S(2)}, u32[]{:S(2)}) async-start(f32[8,1272,256]{2,1,0:T(8,128)} %bitcast.63), calls=%async_computation.6 | async-start | bytes 20840448 | tf_op jit(solution)/shard_map/all_to_all | solution.py:147
  885.2 65.0 %all-to-all-start.9 = ((f32[8,1272,128]{2,1,0:T(8,128)}), f32[8,1272,128]{2,1,0:T(8,128)}, u32[]{:S(2)}, u32[]{:S(2)}) async-start(f32[8,1272,128]{2,1,0:T(8,128)} %bitcast.72), calls=%async_computation.11 | async-start | bytes 10420224 | tf_op jit(solution)/shard_map/all_to_all | solution.py:147
  950.3 121.0 %all-to-all-start.11 = ((f32[8,1272,256]{2,1,0:T(8,128)}), f32[8,1272,256]{2,1,0:T(8,128)}, u32[]{:S(2)}, u32[]{:S(2)}) async-start(f32[8,1272,256]{2,1,0:T(8,128)} %bitcast.65), calls=%async_computation.15 | async-start | bytes 20840448 | tf_op jit(solution)/shard_map/all_to_all | solution.py:147
  955.5 731.0 %reduce-scatter.10.cloned.1.call-start = ((), (), s32[]{:S(2)}) async-start(), calls=%async_computation.25 | async-start | bytes 3932160 | tf_op jit(solution)/shard_map/reduce_scatter | solution.py:153
  1012.6 673.9 %reduce-scatter.14.cloned.1.call-start = ((), (), s32[]{:S(2)}) async-start(), calls=%async_computation.27 | async-start | bytes 7864320 | tf_op jit(solution)/shard_map/reduce_scatter | solution.py:153
  1124.7 561.9 %reduce-scatter.12.cloned.1.call-start = ((), (), s32[]{:S(2)}) async-start(), calls=%async_computation.26 | async-start | bytes 7864320 | tf_op jit(solution)/shard_map/reduce_scatter | solution.py:153
  1338.4 359.3 %reduce-scatter.6.cloned.1.call-start = ((), (), s32[]{:S(2)}) async-start(), calls=%async_computation.23 | async-start | bytes 7864320 | tf_op jit(solution)/shard_map/reduce_scatter | solution.py:153
  1487.4 359.6 %reduce-scatter.8.cloned.1.call-start = ((), (), s32[]{:S(2)}) async-start(), calls=%async_computation.24 | async-start | bytes 11796480 | tf_op jit(solution)/shard_map/reduce_scatter | solution.py:153
  (4 other events, 5.3 us)
Sparse Core Ops, SparseCore 0:
  14.7 61.8 all-gather.6
  78.2 63.1 all-gather.12
  142.9 113.5 all-gather.10
  258.5 113.4 all-gather.8
  374.0 113.5 all-gather.14
  489.6 113.5 all-gather.16
  1012.8 60.7 reduce-scatter.9
  1124.8 109.5 reduce-scatter.13
  1338.6 109.4 reduce-scatter.11
  1487.5 109.5 reduce-scatter.5
  1686.6 160.3 reduce-scatter.7
